TPU v7x, 128 devices: a whole 4x4x4 slice. The times are simulated.
128 devices in a mesh: px: 16 (over y, z_hi, core), py: 8 (over x, z_lo).
Axes of the slice: x: 4, y: 4, z: 4 (z_hi: 2, z_lo: 2; z = z_hi * 2 + z_lo), core: 2. Of those that a mesh axis runs over, the one named last changes fastest.
Arguments:
- source: float32 [1024, 512, 128], P('px', 'py'), may hold values from -8 to 8
- layer_mass: float32 [128], replicated, may hold values from 0.5 to 4
- modes: float32 [128, 128], replicated, may hold values from -0.5 to 0.5
- mode_eigen: float32 [128], replicated, may hold values from 0.0002 to 1
Outputs:
- solution: float32 [1024, 512, 128], P('px', 'py')
All inputs are finite; a program needn't handle non-finite values.
Results may differ from a plain program's by a relative error of at most 0.0014.
Values sent between devices are 32-bit elements; how exact they have to be, the bound alone decides.
No kernel may reach another device: no remote copies, remote signals or barrier semaphores. Data moves between devices by JAX's collectives and lax.ppermute only.
A program may use at most 64 MiB of HBM per device.

v0:
```python
import jax
import jax.numpy as jnp
import numpy as np
from jax import lax
from jax.experimental import pallas as pl
from jax.experimental.pallas import tpu as pltpu
from jax.sharding import PartitionSpec as P

NX, NY, NZ = 1024, 512, 128
PX, PY = 16, 8
T = 64
H = T // 2
F32 = jnp.float32
BF16 = jnp.bfloat16
AXES = ("px", "py")


def np_split(table):
    table = np.asarray(table, np.float64)
    high = table.astype(np.float32).astype(jnp.bfloat16)
    low = (table - high.astype(np.float64)).astype(np.float32).astype(jnp.bfloat16)
    return high, low


def pair(table):
    return np.stack(np_split(table))


def sine_table():
    a = np.arange(1, T + 1)
    return np.sqrt(2.0 / (T + 1)) * np.sin(np.pi * np.outer(a, a) / (T + 1))


SINE = sine_table()
EDGE = SINE[:, 0]
LAM_T = 2.0 - 2.0 * np.cos(np.pi * np.arange(1, T + 1) / (T + 1))
ORDER_A = np.concatenate([np.arange(0, T, 2), np.arange(1, T, 2)])


def norm_row(length):
    return np.where(np.arange(length) == 0, np.sqrt(1.0 / length), np.sqrt(2.0 / length))


def tile_tables():
    ky = np.kron(np.eye(4), SINE)
    kx = np.stack([pair(np.kron(SINE[p::2, :H], np.eye(8))) for p in range(2)])
    kxt = np.stack([pair(np.kron(SINE[p::2, :H].T, np.eye(8))) for p in range(2)])
    edge_b = np.broadcast_to(EDGE[:, None], (T, NZ)).astype(np.float32)
    lam_b = np.broadcast_to(LAM_T[:, None], (T, NZ)).astype(np.float32)
    rows = np.stack([np.ones(8), (-1.0) ** np.arange(8)])
    ysel = np.concatenate([np.kron(np.eye(H), rows[s : s + 1]) for s in range(2)])
    return pair(ky), kx, kxt, np.stack([edge_b, lam_b]), ysel.astype(jnp.bfloat16)


def solve_tables():
    al, be = np.arange(NX), np.arange(NY)
    sx, sy = norm_row(NX), norm_row(NY)
    local = np.arange(T) + 0.5
    lines_x = np.stack([T * np.arange(PX) - 0.5, T * np.arange(PX) + T + 0.5])
    lines_y = np.stack([T * np.arange(PY) - 0.5, T * np.arange(PY) + T + 0.5])
    bkx = sx[:, None] * np.cos(np.pi * al[:, None] * lines_x.reshape(1, -1) / NX)
    bky = sy[:, None] * np.cos(np.pi * be[:, None] * lines_y.reshape(1, -1) / NY)
    bky = bky.reshape(NY, 2, 1, PY)
    bys = np.broadcast_to(bky, (NY, 2, PX, PY)).reshape(NY, 2 * PX * PY).T
    place = np.arange(NY) + 0.5
    cy = sy[:, None] * np.cos(np.pi * be[:, None] * place[None] / NY)
    cyl = np.einsum("bpy,cy->pcb", cy.reshape(NY, PY, T), SINE).reshape(NY, NY)
    phase = np.pi * al[:, None] * local[None] / NX
    m1 = (sx[:, None] * np.cos(phase)) @ SINE[:, ORDER_A]
    m2 = (sx[:, None] * np.sin(phase)) @ SINE[:, ORDER_A]
    turn = np.pi * np.arange(32)[:, None] * np.arange(PX)[None] / PX
    wide = lambda t: np.tile(np.repeat(t, PY, axis=1), (1, 2))
    turns = np.stack([wide(np.cos(turn)), wide(np.sin(turn))]).astype(np.float32)
    lam_x = (2.0 - 2.0 * np.cos(np.pi * al / NX)).astype(np.float32)[:, None]
    lam_y = (2.0 - 2.0 * np.cos(np.pi * be / NY)).astype(np.float32)[None]
    m12 = np.stack([pair(m1), pair(m2)])
    m12t = np.stack([pair(m1.T), pair(-m2.T)])
    return pair(bkx), pair(bkx.T), pair(bys), pair(cyl), m12, m12t, turns, lam_x, lam_y


def split(value):
    high = value.astype(BF16)
    return high, (value - high.astype(F32)).astype(BF16)


def dot(a, b, dims=(((1,), (0,)), ((), ()))):
    return lax.dot_general(a, b, dims, preferred_element_type=F32)


NT = (((1,), (1,)), ((), ()))


def dot3(a, b, dims=(((1,), (0,)), ((), ()))):
    return dot(a[0], b[0], dims) + dot(a[0], b[1], dims) + dot(a[1], b[0], dims)


def block_diag2(w):
    zero = jnp.zeros_like(w)
    top = jnp.concatenate([w, zero], axis=1)
    bottom = jnp.concatenate([zero, w], axis=1)
    return jnp.concatenate([top, bottom], axis=0)


def two(ref, *index):
    return ref[(*index, 0)], ref[(*index, 1)]


def forward_kernel(src, mass, modes, eig, ky, kx, rowtab, ysel, coef, edges, ybuf):
    w = split(mass[...] * modes[...])
    w = block_diag2(w[0]), block_diag2(w[1])
    kyp = two(ky)
    for g in range(8):
        near = src[4 * g : 4 * g + 4].reshape(4 * T, NZ)
        far = jnp.concatenate([src[63 - 4 * g - i] for i in range(4)], axis=0)
        folded = split(jnp.concatenate([near + far, near - far], axis=1))
        modal = split(dot3(folded, w))
        ybuf[4 * g : 4 * g + 4] = dot3(kyp, modal).reshape(4, T, 2 * NZ)
    eig_row = eig[...]
    across = [[None] * 8, [None] * 8]
    along = []
    for p in range(2):
        kxp = two(kx, p)
        acc_y = [None] * H
        for q in range(4):
            parts = [
                ybuf[:, 8 * o : 8 * o + 8, p * NZ : (p + 1) * NZ].reshape(8 * H, NZ)
                for o in (2 * q, 2 * q + 1)
            ]
            spec = dot3(kxp, split(jnp.concatenate(parts, axis=1)))
            for i in range(2):
                o = 2 * q + i
                block = spec[:, i * NZ : (i + 1) * NZ]
                coef[p, :, 8 * o : 8 * o + 8, :] = block.reshape(H, 8, NZ)
                base = eig_row + rowtab[1, 8 * o : 8 * o + 8, :]
                edge_b = rowtab[0, 8 * o : 8 * o + 8, :]
                acc_x = None
                for j in range(H):
                    a = 2 * j + p
                    v = block[8 * j : 8 * j + 8] / (base + float(LAM_T[a]))
                    vx = v * float(EDGE[a])
                    vy = v * edge_b
                    acc_x = vx if acc_x is None else acc_x + vx
                    acc_y[j] = vy if acc_y[j] is None else acc_y[j] + vy
                across[p][o] = acc_x
        along.append(jnp.concatenate(acc_y, axis=0))
    even = jnp.concatenate(across[0], axis=0)
    odd = jnp.concatenate(across[1], axis=0)
    sums = split(jnp.concatenate(along, axis=1))
    sel = ysel[...]
    ends = dot(sel, sums[0]) + dot(sel, sums[1])
    first = jnp.concatenate([ends[:H, :NZ], ends[:H, NZ:]], axis=0)
    last = jnp.concatenate([ends[H:, :NZ], ends[H:, NZ:]], axis=0)
    xs = jnp.concatenate([even + odd, even - odd], axis=0)
    ys = jnp.concatenate([first, last], axis=0)
    edges[:, 0, 0:NZ] = xs.T
    edges[:, 0, NZ : 2 * NZ] = ys.T


def interface_kernel(
    got, eig, bkx, bkxt, bys, cyl, m12, m12t, turns, lam_x, lam_y, out, xbuf
):
    mode = lax.axis_index("px") * PY + lax.axis_index("py")
    mu = eig[mode]
    lane = lax.broadcasted_iota(jnp.int32, (2 * PX, NZ), 1)
    low_half = lane < T
    xbuf[...] = got[:, 0, 0:NZ]
    tiles = []
    for q in range(4):
        rows = []
        for i in range(2):
            d = xbuf[pl.ds(2 * q + i, PX, stride=PY), :]
            swapped = pltpu.roll(d, T, 1)
            rows.append(jnp.concatenate([d, swapped] if i == 0 else [swapped, d], axis=0))
        tiles.append(jnp.where(low_half, rows[0], rows[1]))
    lines = jnp.concatenate(tiles, axis=1)
    cylp = two(cyl)
    t1 = split(dot3(split(lines), cylp))
    ends = got[:, 0, NZ : 2 * NZ].T
    ends = jnp.concatenate([ends[:T], ends[T:]], axis=1)
    endsp = split(ends)
    bysp = two(bys)
    cos_t = turns[0]
    sin_t = turns[1]
    shift = lam_y[...] + mu
    back_x = None
    back_y = None
    for c in range(4):
        rows = slice(256 * c, 256 * c + 256)
        m1 = m12[0, 0, rows], m12[0, 1, rows]
        m2 = m12[1, 0, rows], m12[1, 1, rows]
        z1 = dot3(m1, endsp).reshape(8, 32, 256) * cos_t[None]
        z2 = dot3(m2, endsp).reshape(8, 32, 256) * sin_t[None]
        z = split((z1 - z2).reshape(256, 256))
        spec = dot3((bkx[0, rows], bkx[1, rows]), t1) + dot3(z, bysp)
        u = split(spec / (shift + lam_x[rows]))
        bx = dot3((bkxt[0, :, rows], bkxt[1, :, rows]), u)
        back_x = bx if back_x is None else back_x + bx
        r = dot3(u, bysp, NT).reshape(8, 32, 256)
        r1 = split((r * cos_t[None]).reshape(256, 256))
        r2 = split((r * sin_t[None]).reshape(256, 256))
        by = dot3((m12t[0, 0, :, rows], m12t[0, 1, :, rows]), r1)
        by += dot3((m12t[1, 0, :, rows], m12t[1, 1, :, rows]), r2)
        back_y = by if back_y is None else back_y + by
    wx = dot3(split(back_x), cylp, NT)
    row = lax.broadcasted_iota(jnp.int32, (PX, NY), 0)
    before, after = lines[:PX], lines[PX:]
    wx0 = wx[:PX] + jnp.where(row == 0, before, pltpu.roll(after, 1, 0))
    wx1 = wx[PX:] + jnp.where(row == PX - 1, after, pltpu.roll(before, PX - 1, 0))
    low16 = low_half[:PX]
    for q in range(4):
        w0 = wx0[:, q * NZ : (q + 1) * NZ]
        w1 = wx1[:, q * NZ : (q + 1) * NZ]
        xbuf[pl.ds(2 * q, PX, stride=PY), :] = jnp.where(low16, w0, pltpu.roll(w1, T, 1))
        xbuf[pl.ds(2 * q + 1, PX, stride=PY), :] = jnp.where(low16, pltpu.roll(w0, T, 1), w1)
    out[:, 0, 0:NZ] = xbuf[...]
    col = lax.broadcasted_iota(jnp.int32, (T, NZ), 1) % PY
    before, after = ends[:, :NZ], ends[:, NZ:]
    wy0 = back_y[:, :NZ] + jnp.where(col == 0, before, pltpu.roll(after, 1, 1))
    wy1 = back_y[:, NZ:] + jnp.where(col == PY - 1, after, pltpu.roll(before, NZ - 1, 1))
    out[:, 0, NZ : 2 * NZ] = jnp.concatenate([wy0, wy1], axis=0).T


def backward_kernel(coef, got, modes, eig, ky, kxt, rowtab, dest, ybuf, qbuf):
    qbuf[0:NZ] = got[:, 0, 0:NZ].T
    qbuf[NZ : 2 * NZ] = got[:, 0, NZ : 2 * NZ].T
    eig_row = eig[...]
    sign = jnp.where(lax.broadcasted_iota(jnp.int32, (8, NZ), 0) % 2 == 0, 1.0, -1.0)
    w = split(modes[...].T)
    w = block_diag2(w[0]), block_diag2(w[1])
    for p in range(2):
        kxp = two(kxt, p)
        ends = [
            qbuf[NZ + p * H + j : NZ + p * H + j + 1] + sign * qbuf[NZ + T + p * H + j : NZ + T + p * H + j + 1]
            for j in range(H)
        ]
        for q in range(4):
            parts = []
            for o in (2 * q, 2 * q + 1):
                near = qbuf[8 * o : 8 * o + 8]
                far = qbuf[T + 8 * o : T + 8 * o + 8]
                line = near + far if p == 0 else near - far
                base = eig_row + rowtab[1, 8 * o : 8 * o + 8, :]
                edge_b = rowtab[0, 8 * o : 8 * o + 8, :]
                blocks = []
                for j in range(H):
                    a = 2 * j + p
                    r = coef[p, j, 8 * o : 8 * o + 8, :] + line * float(EDGE[a]) + ends[j] * edge_b
                    blocks.append(r / (base + float(LAM_T[a])))
                parts.append(jnp.concatenate(blocks, axis=0))
            back = dot3(kxp, split(jnp.concatenate(parts, axis=1)))
            for i in range(2):
                o = 2 * q + i
                ybuf[:, 8 * o : 8 * o + 8, p * NZ : (p + 1) * NZ] = back[
                    :, i * NZ : (i + 1) * NZ
                ].reshape(H, 8, NZ)
    kyp = two(ky)
    for g in range(8):
        block = split(ybuf[4 * g : 4 * g + 4].reshape(4 * T, 2 * NZ))
        modal = split(dot3(kyp, block))
        res = dot3(modal, w)
        near = res[:, :NZ]
        far = res[:, NZ:]
        dest[4 * g : 4 * g + 4] = (near + far).reshape(4, T, NZ)
        other = near - far
        for i in range(4):
            dest[63 - 4 * g - i] = other[T * i : T * i + T]


VMEM = pl.BlockSpec(memory_space=pltpu.VMEM)
SMEM = pl.BlockSpec(memory_space=pltpu.SMEM)
INTERPRET = False


def shards(source, layer_mass, modes, mode_eigen):
    ky, kx, kxt, rowtab, ysel = tile_tables()
    params = pltpu.CompilerParams(vmem_limit_bytes=48 * 1024 * 1024)
    coef, edges = pl.pallas_call(
        forward_kernel,
        out_shape=(
            jax.ShapeDtypeStruct((2, H, T, NZ), F32),
            jax.ShapeDtypeStruct((NZ, 1, 2 * NZ), F32),
        ),
        in_specs=[VMEM] * 8,
        out_specs=(VMEM, VMEM),
        scratch_shapes=[pltpu.VMEM((H, T, 2 * NZ), F32)],
        compiler_params=params,
        interpret=INTERPRET,
        name="forward",
    )(source, layer_mass[:, None], modes, mode_eigen[None], ky, kx, rowtab, ysel)
    edges = lax.all_to_all(edges, AXES, split_axis=0, concat_axis=0, tiled=True)
    values = pl.pallas_call(
        interface_kernel,
        out_shape=jax.ShapeDtypeStruct((NZ, 1, 2 * NZ), F32),
        in_specs=[VMEM, SMEM] + [VMEM] * 9,
        out_specs=VMEM,
        scratch_shapes=[pltpu.VMEM((NZ, NZ), F32)],
        compiler_params=params,
        interpret=INTERPRET,
        name="interface",
    )(edges, mode_eigen, *solve_tables())
    values = lax.all_to_all(values, AXES, split_axis=0, concat_axis=0, tiled=True)
    return pl.pallas_call(
        backward_kernel,
        out_shape=jax.ShapeDtypeStruct((T, T, NZ), F32),
        in_specs=[VMEM] * 7,
        out_specs=VMEM,
        scratch_shapes=[pltpu.VMEM((H, T, 2 * NZ), F32), pltpu.VMEM((2 * NZ, NZ), F32)],
        compiler_params=params,
        interpret=INTERPRET,
        name="backward",
    )(coef, values, modes, mode_eigen[None], ky, kxt, rowtab)


def solution(mesh):
    placed = (P("px", "py", None), P(), P(), P())
    return jax.shard_map(
        shards, mesh=mesh, in_specs=placed, out_specs=P("px", "py", None), check_vma=False
    )
```

profile of v0, /device:TPU:1, one launch (start us, length us, event | category | flops | bytes accessed | tf_op | source)
XLA Modules:
  0.0 61.5 jit_solution(8445531342995155567)
XLA Ops:
  0.0 0.0 copy-start.16
  0.0 0.0 copy-start.13
  0.0 0.8 %copy.19.mass = f32[128,1]{1,0:T(8,128)S(1)} copy(f32[128,1]{0,1:T(1,128)} %bitcast.4) | data formatting | bytes 1024 | tf_op jit(solution)/shard_map/broadcast_in_dim | solution.py:289
  0.8 0.0 copy-start
  0.8 1.6 %copy-done = f32[64,64,128]{2,1,0:T(8,128)S(1)} copy-done((f32[64,64,128]{2,1,0:T(8,128)S(1)}, f32[64,64,128]{2,1,0:T(8,128)}, u32[]{:S(2)}) %copy-start) | copy-done | bytes 2097176
  2.4 0.0 copy-start.3
  2.4 0.9 %copy-done.3 = bf16[2,256,256]{2,1,0:T(8,128)(2,1)S(1)} copy-done((bf16[2,256,256]{2,1,0:T(8,128)(2,1)S(1)}, bf16[2,256,256]{2,1,0:T(8,128)(2,1)}, u32[]{:S(2)}) %copy-start.3) | copy-done | bytes 262168
  3.3 0.0 copy-start.8
  3.3 1.0 %copy-done.8 = bf16[2,2,256,256]{3,2,1,0:T(8,128)(2,1)S(1)} copy-done((bf16[2,2,256,256]{3,2,1,0:T(8,128)(2,1)S(1)}, bf16[2,2,256,256]{3,2,1,0:T(8,128)(2,1)}, u32[]{:S(2)}) %copy-start.8) | copy-done | bytes 524312
  4.4 0.0 copy-start.10
  4.4 0.8 %copy-done.10 = f32[128,128]{1,0:T(8,128)S(1)} copy-done((f32[128,128]{1,0:T(8,128)S(1)}, f32[128,128]{1,0:T(8,128)}, u32[]{:S(2)}) %copy-start.10) | copy-done | bytes 65560
  5.2 0.0 copy-start.11
  5.2 0.8 %copy-done.11 = f32[2,64,128]{2,1,0:T(8,128)S(1)} copy-done((f32[2,64,128]{2,1,0:T(8,128)S(1)}, f32[2,64,128]{2,1,0:T(8,128)}, u32[]{:S(2)}) %copy-start.11) | copy-done | bytes 65560
  6.1 0.0 copy-start.14
  6.1 0.8 %copy-done.14 = bf16[64,256]{1,0:T(8,128)(2,1)S(1)} copy-done((bf16[64,256]{1,0:T(8,128)(2,1)S(1)}, bf16[64,256]{1,0:T(8,128)(2,1)}, u32[]{:S(2)}) %copy-start.14) | copy-done | bytes 32792
  6.8 0.0 copy-start.15
  6.8 0.7 %copy-done.15 = f32[128]{0:T(128)S(1)} copy-done((f32[128]{0:T(128)S(1)}, f32[128]{0:T(128)}, u32[]{:S(2)}) %copy-start.15) | copy-done | bytes 536
  7.5 0.0 copy-start.1
  7.5 0.0 copy-start.2
  7.5 0.0 copy-start.4
  7.5 0.0 copy-start.5
  7.5 0.0 copy-start.12
  7.5 3.5 %forward.1 = (f32[2,32,64,128]{3,2,1,0:T(8,128)S(1)}, f32[128,1,256]{2,1,0:T(1,128)S(1)}) custom-call(f32[64,64,128]{2,1,0:T(8,128)S(1)} %copy-done, f32[128,1]{1,0:T(8,128)S(1)} %copy.19.mass, f32[128,128]{1,0:T(8,128)S(1)} %copy-done.10, f32[1,128]{1,0:T(1,128)S(1)} %bitcast.2, bf16[2,256,256]{2,1,0:T(8,128)(2,1)S(1)} %copy-done.3, ...), custom_call_target="tpu_custom_call" | custom-call | tf_op jit(solution)/shard_map/forward/pallas_call | solution.py:277
  11.0 21.3 %all_to_all.10.got = f32[128,1,256]{2,1,0:T(1,128)S(1)} all-to-all(f32[128,1,256]{2,1,0:T(1,128)S(1)} %get-tuple-element.8), channel_id=1, replica_groups=mesh['px'=16,'py'=8] {'px','py'}, dimensions={0} | all-to-all | bytes 262144 | tf_op jit(solution)/shard_map/all_to_all | solution.py:290
  32.3 0.0 copy-done.16
  32.3 0.0 copy-done.13
  32.3 0.0 copy-done.1
  32.3 0.0 copy-done.2
  32.3 0.0 copy-done.4
  32.3 0.0 copy-done.5
  32.3 0.0 copy-done.12
  32.3 0.0 copy-start.6
  32.4 1.0 %copy-done.6 = bf16[2,256,512]{2,1,0:T(8,128)(2,1)S(1)} copy-done((bf16[2,256,512]{2,1,0:T(8,128)(2,1)S(1)}, bf16[2,256,512]{2,1,0:T(8,128)(2,1)}, u32[]{:S(2)}) %copy-start.6) | copy-done | bytes 524312
  33.4 0.0 copy-start.7
  33.4 1.0 %copy-done.7 = bf16[2,1024,32]{2,1,0:T(8,128)(2,1)S(1)} copy-done((bf16[2,1024,32]{2,1,0:T(8,128)(2,1)S(1)}, bf16[2,1024,32]{2,1,0:T(8,128)(2,1)}, u32[]{:S(2)}) %copy-start.7) | copy-done | bytes 131096
  34.4 0.0 copy-start.9
  34.4 8.2 %interface.1 = f32[128,1,256]{2,1,0:T(1,128)S(1)} custom-call(f32[128,1,256]{2,1,0:T(1,128)S(1)} %all_to_all.10.got, f32[128]{0:T(128)S(1)} %copy-done.15, bf16[2,1024,32]{2,1,0:T(8,128)(2,1)S(1)} %copy-done.7, bf16[2,32,1024]{2,1,0:T(8,128)(2,1)S(1)} %copy-done.12, bf16[2,256,512]{2,1,0:T(8,128)(2,1)S(1)} %copy-done.6, bf16[2,512,512]{2,1,0:T(8,128)(2,1)S(1)} %copy-done.2, ...), custom_call_target="tpu_custom_call" | custom-call | tf_op jit(solution)/shard_map/interface/pallas_call | solution.py:291
  42.6 14.2 %all_to_all.11.got = f32[128,1,256]{2,1,0:T(1,128)S(1)} all-to-all(f32[128,1,256]{2,1,0:T(1,128)S(1)} %interface.1), channel_id=1, replica_groups=mesh['px'=16,'py'=8] {'px','py'}, dimensions={0} | all-to-all | bytes 262144 | tf_op jit(solution)/shard_map/all_to_all | solution.py:301
  56.8 0.0 copy-done.9
  56.8 4.7 %backward.1 = f32[64,64,128]{2,1,0:T(8,128)} custom-call(f32[2,32,64,128]{3,2,1,0:T(8,128)S(1)} %get-tuple-element.7.coef, f32[128,1,256]{2,1,0:T(1,128)S(1)} %all_to_all.11.got, f32[128,128]{1,0:T(8,128)S(1)} %copy-done.10, f32[1,128]{1,0:T(1,128)S(1)} %bitcast.3, bf16[2,256,256]{2,1,0:T(8,128)(2,1)S(1)} %copy-done.3, ...), custom_call_target="tpu_custom_call" | custom-call | tf_op jit(solution)/shard_map/backward/pallas_call | solution.py:302
Async XLA Ops:
  0.0 32.3 %copy-start.16 = (f32[1,512]{1,0:T(1,128)S(1)}, f32[1,512]{1,0:T(1,128)}, u32[]{:S(2)}) copy-start(f32[1,512]{1,0:T(1,128)} %constant.40.clone.lam_y) | copy-start | bytes 6148
  0.0 32.3 %copy-start.13 = (f32[2,32,256]{2,1,0:T(8,128)S(1)}, f32[2,32,256]{2,1,0:T(8,128)}, u32[]{:S(2)}) copy-start(f32[2,32,256]{2,1,0:T(8,128)} %constant.38.clone.turns) | copy-start | bytes 196612
  0.8 1.6 %copy-start = (f32[64,64,128]{2,1,0:T(8,128)S(1)}, f32[64,64,128]{2,1,0:T(8,128)}, u32[]{:S(2)}) copy-start(f32[64,64,128]{2,1,0:T(8,128)} %src.1) | copy-start | bytes 6291460
  2.4 0.9 %copy-start.3 = (bf16[2,256,256]{2,1,0:T(8,128)(2,1)S(1)}, bf16[2,256,256]{2,1,0:T(8,128)(2,1)}, u32[]{:S(2)}) copy-start(bf16[2,256,256]{2,1,0:T(8,128)(2,1)} %constant.28.clone.ky) | copy-start | bytes 786436
  3.3 1.0 %copy-start.8 = (bf16[2,2,256,256]{3,2,1,0:T(8,128)(2,1)S(1)}, bf16[2,2,256,256]{3,2,1,0:T(8,128)(2,1)}, u32[]{:S(2)}) copy-start(bf16[2,2,256,256]{3,2,1,0:T(8,128)(2,1)} %constant.29.clone.kx) | copy-start | bytes 1572868
  4.4 0.8 %copy-start.10 = (f32[128,128]{1,0:T(8,128)S(1)}, f32[128,128]{1,0:T(8,128)}, u32[]{:S(2)}) copy-start(f32[128,128]{1,0:T(8,128)} %modes.3) | copy-start | bytes 196612
  5.2 0.8 %copy-start.11 = (f32[2,64,128]{2,1,0:T(8,128)S(1)}, f32[2,64,128]{2,1,0:T(8,128)}, u32[]{:S(2)}) copy-start(f32[2,64,128]{2,1,0:T(8,128)} %constant.30.clone.rowtab) | copy-start | bytes 196612
  6.1 0.8 %copy-start.14 = (bf16[64,256]{1,0:T(8,128)(2,1)S(1)}, bf16[64,256]{1,0:T(8,128)(2,1)}, u32[]{:S(2)}) copy-start(bf16[64,256]{1,0:T(8,128)(2,1)} %constant.31.clone.ysel) | copy-start | bytes 98308
  6.8 0.7 %copy-start.15 = (f32[128]{0:T(128)S(1)}, f32[128]{0:T(128)}, u32[]{:S(2)}) copy-start(f32[128]{0:T(128)} %eig.1) | copy-start | bytes 1540
  7.5 24.8 %copy-start.1 = (bf16[2,2,1024,64]{3,2,1,0:T(8,128)(2,1)S(1)}, bf16[2,2,1024,64]{3,2,1,0:T(8,128)(2,1)}, u32[]{:S(2)}) copy-start(bf16[2,2,1024,64]{3,2,1,0:T(8,128)(2,1)} %constant.36.clone.m12) | copy-start | bytes 1572868
  7.5 24.8 %copy-start.2 = (bf16[2,512,512]{2,1,0:T(8,128)(2,1)S(1)}, bf16[2,512,512]{2,1,0:T(8,128)(2,1)}, u32[]{:S(2)}) copy-start(bf16[2,512,512]{2,1,0:T(8,128)(2,1)} %constant.35.clone.cyl) | copy-start | bytes 3145732
  7.5 24.8 %copy-start.4 = (f32[1024,1]{1,0:T(8,128)S(1)}, f32[1024,1]{1,0:T(8,128)}, u32[]{:S(2)}) copy-start(f32[1024,1]{1,0:T(8,128)} %constant.39.clone.lam_x) | copy-start | bytes 12292
  7.5 24.8 %copy-start.5 = (bf16[2,2,64,1024]{3,2,1,0:T(8,128)(2,1)S(1)}, bf16[2,2,64,1024]{3,2,1,0:T(8,128)(2,1)}, u32[]{:S(2)}) copy-start(bf16[2,2,64,1024]{3,2,1,0:T(8,128)(2,1)} %constant.37.clone.m12t) | copy-start | bytes 1572868
  7.5 24.8 %copy-start.12 = (bf16[2,32,1024]{2,1,0:T(8,128)(2,1)S(1)}, bf16[2,32,1024]{2,1,0:T(8,128)(2,1)}, u32[]{:S(2)}) copy-start(bf16[2,32,1024]{2,1,0:T(8,128)(2,1)} %constant.33.clone.bkxt) | copy-start | bytes 393220
  32.3 1.0 %copy-start.6 = (bf16[2,256,512]{2,1,0:T(8,128)(2,1)S(1)}, bf16[2,256,512]{2,1,0:T(8,128)(2,1)}, u32[]{:S(2)}) copy-start(bf16[2,256,512]{2,1,0:T(8,128)(2,1)} %constant.34.clone.bys) | copy-start | bytes 1572868
  33.4 1.0 %copy-start.7 = (bf16[2,1024,32]{2,1,0:T(8,128)(2,1)S(1)}, bf16[2,1024,32]{2,1,0:T(8,128)(2,1)}, u32[]{:S(2)}) copy-start(bf16[2,1024,32]{2,1,0:T(8,128)(2,1)} %constant.32.clone.bkx) | copy-start | bytes 393220
  34.4 22.4 %copy-start.9 = (bf16[2,2,256,256]{3,2,1,0:T(8,128)(2,1)S(1)}, bf16[2,2,256,256]{3,2,1,0:T(8,128)(2,1)}, u32[]{:S(2)}) copy-start(bf16[2,2,256,256]{3,2,1,0:T(8,128)(2,1)} %constant.41.clone.kxt) | copy-start | bytes 1572868
where the time goes:
time: 62 us; the launch traced here: 61.5 us
  blocking collectives  35.5 us (57%)
  Pallas kernels  16.3 us (26%)
  local copies, waits for them, and re-layouts  9.57 us (15%)
    all_to_all x1, blocking collectives, shards(): edges = lax.all_to_all(edges, AXES, split_axis=0, concat_axis=0, tiled=True)  21.3 us
    all_to_all x1, blocking collectives, shards(): lax.all_to_all(values, AXES, split_axis=0, concat_axis=0, tiled=True)  14.2 us
    unnamed x34, local copies, waits for them, and re-layouts  8.78 us
    pallas_call x1, Pallas kernels, shards(): pl.pallas_call(interface_kernel, out_shape=jax.ShapeDtypeStruct((NZ, 1, 2...  8.19 us
    pallas_call x1, Pallas kernels, shards(): pl.pallas_call(backward_kernel, out_shape=jax.ShapeDtypeStruct((T, T, NZ)...  4.65 us
    pallas_call x1, Pallas kernels, shards(): pl.pallas_call(forward_kernel, out_shape=(jax.ShapeDtypeStruct((2, H, T,...  3.5 us

commit v1 on v0

v1 whole, which is shorter than its diff:
```python
import jax
import jax.numpy as jnp
import numpy as np
from jax import lax
from jax.experimental import pallas as pl
from jax.experimental.pallas import tpu as pltpu
from jax.sharding import PartitionSpec as P

NX, NY, NZ = 1024, 512, 128
PX, PY = 16, 8
T = 64
H = T // 2
F32 = jnp.float32
BF16 = jnp.bfloat16
AXES = ("px", "py")


def np_split(table):
    table = np.asarray(table, np.float64)
    high = table.astype(np.float32).astype(jnp.bfloat16)
    low = (table - high.astype(np.float64)).astype(np.float32).astype(jnp.bfloat16)
    return high, low


def pair(table):
    return np.stack(np_split(table))


def sine_table():
    a = np.arange(1, T + 1)
    return np.sqrt(2.0 / (T + 1)) * np.sin(np.pi * np.outer(a, a) / (T + 1))


SINE = sine_table()
EDGE = SINE[:, 0]
LAM_T = 2.0 - 2.0 * np.cos(np.pi * np.arange(1, T + 1) / (T + 1))
ORDER_A = np.concatenate([np.arange(0, T, 2), np.arange(1, T, 2)])


def norm_row(length):
    return np.where(np.arange(length) == 0, np.sqrt(1.0 / length), np.sqrt(2.0 / length))


def tile_tables():
    rows = [SINE[p::2, :H] for p in range(2)] + [SINE[p::2, :H].T for p in range(2)]
    spread = np.concatenate([np.repeat(r, 8, axis=1) for r in rows])
    small = np.concatenate([spread, np.tile(SINE, (1, 4))]).astype(np.float32)
    edge_b = np.broadcast_to(EDGE[:, None], (T, NZ))
    lam_b = np.broadcast_to(LAM_T[:, None], (T, NZ))
    rowtab = np.concatenate([edge_b, lam_b]).astype(np.float32)
    signs = np.stack([np.ones(8), (-1.0) ** np.arange(8)])
    ysel = np.concatenate([np.kron(np.eye(H), signs[s : s + 1]) for s in range(2)])
    return small, rowtab, ysel.astype(jnp.bfloat16)


def solve_tables():
    al, be = np.arange(NX), np.arange(NY)
    sx, sy = norm_row(NX), norm_row(NY)
    by_parity = lambda n: np.concatenate([np.arange(0, n, 2), np.arange(1, n, 2)])
    al, be = by_parity(NX), by_parity(NY)
    sx, sy = sx[al], sy[be]
    local = np.arange(T) + 0.5
    lines_x = T * np.arange(PX) - 0.5
    lines_y = np.stack([T * np.arange(PY) - 0.5, T * np.arange(PY) + T + 0.5])
    bkx = sx[:, None] * np.cos(np.pi * al[:, None] * lines_x[None] / NX)
    bky = sy[:, None] * np.cos(np.pi * be[:, None] * lines_y.reshape(1, -1) / NY)
    bky = bky.reshape(NY, 2, 1, PY)
    bys = np.broadcast_to(bky, (NY, 2, PX // 2, PY)).reshape(NY, PX * PY).T
    place = np.arange(NY // 2) + 0.5
    cy = sy[:, None] * np.cos(np.pi * be[:, None] * place[None] / NY)
    cyl = np.einsum("bpy,cy->pcb", cy.reshape(NY, PY // 2, T), SINE).reshape(NY // 2, NY)
    cyl = np.stack([pair(cyl[:, : NY // 2]), pair(cyl[:, NY // 2 :])])
    phase = np.pi * al[:, None] * local[None] / NX
    m1 = (sx[:, None] * np.cos(phase)) @ SINE[:, ORDER_A]
    m2 = (sx[:, None] * np.sin(phase)) @ SINE[:, ORDER_A]
    m12 = np.concatenate(np_split(np.concatenate([m1, m2], axis=1)), axis=1)
    lam_x = 2.0 - 2.0 * np.cos(np.pi * al / NX)
    lam_h, lam_l = np_split(lam_x)
    rest = lam_x - lam_h.astype(np.float64) - lam_l.astype(np.float64)
    bkx_h, bkx_l = np_split(bkx)
    lams = np.stack([lam_h, lam_l, np_split(rest)[0]], axis=1)
    bkx_all = np.zeros((NX, 128), jnp.bfloat16)
    for i, part in enumerate((bkx_h, bkx_l, bkx_h, lams)):
        bkx_all[:, 16 * i : 16 * i + part.shape[1]] = part
    bkxt = np.stack([pair(bkx[512 * p : 512 * p + 512].T) for p in range(2)])
    px = np.arange(PX // 2)
    tz, tr = [], []
    for p in range(2):
        turn = np.pi * (2 * np.arange(16) + p)[:, None] * px[None] / PX
        wide = [np.tile(np.repeat(t, PY, axis=1), (1, 2)) for t in (np.cos(turn), -np.sin(turn))]
        tz.append(np.concatenate(wide, axis=1))
        tr += [np.tile(t.T, (1, 8)) for t in wide]
    tz = np.concatenate(tz).astype(np.float32)
    tr = np.stack(tr).astype(np.float32)
    lam_y = (2.0 - 2.0 * np.cos(np.pi * be / NY)).astype(np.float32)[None]
    return cyl, m12, bkx_all, bkxt, pair(bys), tz, tr, lam_y


def split(value):
    high = value.astype(BF16)
    return high, (value - high.astype(F32)).astype(BF16)


PLAIN = (((1,), (0,)), ((), ()))
NT = (((1,), (1,)), ((), ()))


def dot(a, b, dims=PLAIN):
    return lax.dot_general(a, b, dims, preferred_element_type=F32)


def dot3(a, b, dims=PLAIN):
    return dot(a[0], b[0], dims) + dot(a[0], b[1], dims) + dot(a[1], b[0], dims)


def block_diag2(w):
    zero = jnp.zeros_like(w)
    top = jnp.concatenate([w, zero], axis=1)
    bottom = jnp.concatenate([zero, w], axis=1)
    return jnp.concatenate([top, bottom], axis=0)


def two(ref, *index):
    return ref[(*index, 0)], ref[(*index, 1)]


def lanes(shape, axis):
    return lax.broadcasted_iota(jnp.int32, shape, axis)


def forward_kernel(*refs):
    src_in, mass_in, modes_in, eig_in, small_in, rowtab_in, ysel_in = refs[:7]
    tables_in = refs[7:15]
    coef, edges, ky, kxt, modes, eig, rowtab = refs[15:22]
    tables = refs[22:30]
    src, mass, small, ysel, kx, ybuf, sems = refs[30:]
    jobs = [(small_in, small), (mass_in, mass), (modes_in, modes)]
    for g in range(8):
        for lo in (4 * g, 60 - 4 * g):
            jobs.append((src_in.at[lo : lo + 4], src.at[lo : lo + 4]))
    jobs += [(eig_in, eig), (rowtab_in, rowtab), (ysel_in, ysel)]
    jobs += list(zip(tables_in, tables))
    copies = [pltpu.make_async_copy(a, b, sems.at[i]) for i, (a, b) in enumerate(jobs)]
    for copy in copies:
        copy.start()
    for copy in copies[:3]:
        copy.wait()
    row_block = lanes((T, 4 * T), 1) // T
    for i in range(4):
        part = split(jnp.where(row_block == i, small[4 * H : 4 * H + T, :], 0.0))
        for h in range(2):
            ky[h, T * i : T * i + T, :] = part[h]
    diagonal = lanes((8, 8 * H), 1) % 8 == lanes((8, 8 * H), 0)
    for t in range(4):
        spread = [
            jnp.where(diagonal, small[H * t + j : H * t + j + 1, :], 0.0) for j in range(H)
        ]
        part = split(jnp.concatenate(spread, axis=0))
        for h in range(2):
            if t < 2:
                kx[t, h] = part[h]
            else:
                kxt[t - 2, h] = part[h]
    mass_col = jnp.broadcast_to(mass[...], (NZ, NZ)).T
    w = split(mass_col * modes[...])
    w = block_diag2(w[0]), block_diag2(w[1])
    kyp = two(ky)
    for g in range(8):
        for copy in copies[3 + 2 * g : 5 + 2 * g]:
            copy.wait()
        near = src[4 * g : 4 * g + 4].reshape(4 * T, NZ)
        far = jnp.concatenate([src[63 - 4 * g - i] for i in range(4)], axis=0)
        folded = split(jnp.concatenate([near + far, near - far], axis=1))
        modal = split(dot3(folded, w))
        ybuf[4 * g : 4 * g + 4] = dot3(kyp, modal).reshape(4, T, 2 * NZ)
    for copy in copies[19:22]:
        copy.wait()
    eig_row = eig[...]
    across = [[None] * 8, [None] * 8]
    along = []
    for p in range(2):
        kxp = two(kx, p)
        acc_y = [None] * H
        for q in range(4):
            parts = [
                ybuf[:, 8 * o : 8 * o + 8, p * NZ : (p + 1) * NZ].reshape(8 * H, NZ)
                for o in (2 * q, 2 * q + 1)
            ]
            spec = dot3(kxp, split(jnp.concatenate(parts, axis=1)))
            for i in range(2):
                o = 2 * q + i
                block = spec[:, i * NZ : (i + 1) * NZ]
                coef[p, :, 8 * o : 8 * o + 8, :] = block.reshape(H, 8, NZ)
                base = eig_row + rowtab[T + 8 * o : T + 8 * o + 8, :]
                edge_b = rowtab[8 * o : 8 * o + 8, :]
                acc_x = None
                for j in range(H):
                    a = 2 * j + p
                    v = block[8 * j : 8 * j + 8] / (base + float(LAM_T[a]))
                    vx = v * float(EDGE[a])
                    vy = v * edge_b
                    acc_x = vx if acc_x is None else acc_x + vx
                    acc_y[j] = vy if acc_y[j] is None else acc_y[j] + vy
                across[p][o] = acc_x
        along.append(jnp.concatenate(acc_y, axis=0))
    even = jnp.concatenate(across[0], axis=0)
    odd = jnp.concatenate(across[1], axis=0)
    sums = split(jnp.concatenate(along, axis=1))
    sel = ysel[...]
    ends = dot(sel, sums[0]) + dot(sel, sums[1])
    first = jnp.concatenate([ends[:H, :NZ], ends[:H, NZ:]], axis=0)
    last = jnp.concatenate([ends[H:, :NZ], ends[H:, NZ:]], axis=0)
    xs = jnp.concatenate([even + odd, even - odd], axis=0)
    ys = jnp.concatenate([first, last], axis=0)
    edges[:, 0, 0:NZ] = xs.T
    edges[:, 0, NZ : 2 * NZ] = ys.T
    for copy in copies[22:]:
        copy.wait()


def turned(m):
    return jnp.concatenate([m[PY * (PX - 1 - i) : PY * (PX - i)] for i in range(PX)], axis=0)


def swap(m):
    return pltpu.roll(m, T, 1)


def interface_kernel(got, eig, cyl, m12, bkx, bkxt, bys, tz, tr, lam_y, out, xbuf):
    mode = lax.axis_index("px") * PY + lax.axis_index("py")
    mu = jnp.sum(jnp.where(lanes((1, NZ), 1) == mode, eig[...], 0.0), axis=1, keepdims=True)
    lane = lanes((NZ, NZ), 1)
    low = lane < T
    low32 = low[: 2 * PX]
    low16 = low[:PX]
    low64 = low[:T]
    sign_b = jnp.where(lanes((2 * PX, NZ), 1) % 2 == 0, 1.0, -1.0)
    sign_a = jnp.where(lanes((T, NZ), 1) % T < H, 1.0, -1.0)
    gx = got[:, 0, 0:NZ]
    gy = got[:, 0, NZ : 2 * NZ]

    mirror = swap(turned(gx))
    xbuf[...] = jnp.where(low, gx + mirror, swap(gx - mirror))
    tiles = []
    for q in range(4):
        rows = []
        for i in range(2):
            d = xbuf[pl.ds(2 * q + i, PX, stride=PY), :]
            other = swap(d)
            rows.append(jnp.concatenate([d, other] if i == 0 else [other, d], axis=0))
        tiles.append(jnp.where(low32, rows[0], rows[1]))
    flipped = [sign_b * swap(tiles[3 - q]) for q in range(2)]
    line_e = jnp.concatenate([tiles[q] + flipped[q] for q in range(2)], axis=1)
    line_o = jnp.concatenate([tiles[q] - flipped[q] for q in range(2)], axis=1)
    t1 = jnp.concatenate(
        [dot3(split(line_e), two(cyl, 0)), dot3(split(line_o), two(cyl, 1))], axis=1
    )
    t1h, t1l = split(t1)

    back = turned(gy)[:T]
    part_e = gy[:T] + sign_a * back
    part_o = gy[:T] - sign_a * back
    ends = jnp.concatenate(
        [jnp.where(low64, part_e, swap(part_o)), jnp.where(low64, swap(part_e), part_o)], axis=0
    ).T
    by_h, by_l = two(bys)
    by_lh = jnp.concatenate([by_l, by_h], axis=0)
    shift = lam_y[...] + mu
    back_x, back_y = [], []
    for p in range(2):
        e = split(ends[T * p : T * p + T])
        eh, el = block_diag2(e[0]), block_diag2(e[1])
        ehh = jnp.concatenate([eh, eh], axis=0)
        th, tl = t1h[PX * p : PX * p + PX], t1l[PX * p : PX * p + PX]
        pad = jnp.zeros((NZ - 3 * PX, NY), BF16)
        weights = jnp.concatenate([by_h, th, th, tl, pad], axis=0)
        sum_x = sum_y = None
        for c in range(2):
            rows = slice(512 * p + 256 * c, 512 * p + 256 * c + 256)
            m = m12[rows]
            zz = dot(m, ehh) + dot(m[:, :NZ], el)
            zz = (zz.reshape(16, 16, 256) * tz[16 * p : 16 * p + 16][None]).reshape(256, 256)
            zh, zl = split(zz[:, :NZ] + zz[:, NZ:])
            bk = bkx[rows]
            spec = dot(jnp.concatenate([zh, bk], axis=1), weights)
            spec += dot(jnp.concatenate([zh, zl], axis=1), by_lh)
            lams = bk[:, 48:51].astype(F32)
            lam = (lams[:, 2:3] + lams[:, 1:2]) + lams[:, 0:1]
            u = split(spec / (shift + lam))
            cols = slice(256 * c, 256 * c + 256)
            bx = dot3((bkxt[p, 0, :, cols], bkxt[p, 1, :, cols]), u)
            r = dot3((by_h, by_l), u, NT)
            turns = [jnp.concatenate([tr[2 * p + i]] * 2, axis=1) for i in range(2)]
            rh, rl = split(jnp.concatenate([r * turns[0], r * turns[1]], axis=0))
            wide = dot(rh, m)
            by = wide[:, :NZ] + wide[:, NZ:] + dot(rl, m[:, :NZ])
            sum_x = bx if c == 0 else sum_x + bx
            sum_y = by if c == 0 else sum_y + by
        back_x.append(sum_x)
        back_y.append(sum_y[:NZ] + swap(sum_y[NZ:]))

    bx = jnp.concatenate(back_x, axis=0)
    we = dot3(split(bx[:, : NY // 2]), two(cyl, 0), NT)
    wo = dot3(split(bx[:, NY // 2 :]), two(cyl, 1), NT)
    near = we + wo
    far = we - wo
    for q in range(4):
        if q < 2:
            t = near[:, q * NZ : (q + 1) * NZ]
        else:
            t = swap(sign_b * far[:, (3 - q) * NZ : (4 - q) * NZ])
        s0 = t[:PX] + t[PX:]
        s1 = t[:PX] - t[PX:]
        xbuf[pl.ds(2 * q, PX, stride=PY), :] = jnp.where(low16, s0, swap(s1))
        xbuf[pl.ds(2 * q + 1, PX, stride=PY), :] = jnp.where(low16, swap(s0), s1)
    w = xbuf[...]
    other = swap(gx)
    own = jnp.where(
        low,
        jnp.concatenate([gx[:PY], other[:-PY]], axis=0),
        jnp.concatenate([other[PY:], gx[-PY:]], axis=0),
    )
    out[:, 0, 0:NZ] = jnp.where(low, w, turned(w)) + own

    near = back_y[0] + back_y[1]
    far = back_y[0] - back_y[1]
    near = jnp.where(low64, near[:T], swap(near[T:]))
    far = sign_a * jnp.where(low64, far[:T], swap(far[T:]))
    w = jnp.concatenate([near, turned(jnp.concatenate([far, far], axis=0))[:T]], axis=0)
    row = lanes((NZ, NZ), 0) % PY
    other = swap(gy)
    own = jnp.where(
        low,
        jnp.where(row == 0, gy, pltpu.roll(other, 1, 0)),
        jnp.where(row == PY - 1, gy, pltpu.roll(other, NZ - 1, 0)),
    )
    out[:, 0, NZ : 2 * NZ] = w + own


def backward_kernel(coef, got, modes, eig, ky, kxt, rowtab, dest, ybuf, qbuf, obuf, sems):
    qbuf[0:NZ] = got[:, 0, 0:NZ].T
    qbuf[NZ : 2 * NZ] = got[:, 0, NZ : 2 * NZ].T
    eig_row = eig[...]
    sign = jnp.where(lanes((8, NZ), 0) % 2 == 0, 1.0, -1.0)
    w = split(modes[...].T)
    w = block_diag2(w[0]), block_diag2(w[1])
    for p in range(2):
        kxp = two(kxt, p)
        ends = []
        for j in range(H):
            at = NZ + p * H + j
            ends.append(qbuf[at : at + 1] + sign * qbuf[at + T : at + T + 1])
        for q in range(4):
            parts = []
            for o in (2 * q, 2 * q + 1):
                near = qbuf[8 * o : 8 * o + 8]
                far = qbuf[T + 8 * o : T + 8 * o + 8]
                line = near + far if p == 0 else near - far
                base = eig_row + rowtab[T + 8 * o : T + 8 * o + 8, :]
                edge_b = rowtab[8 * o : 8 * o + 8, :]
                blocks = []
                for j in range(H):
                    a = 2 * j + p
                    r = coef[p, j, 8 * o : 8 * o + 8, :] + line * float(EDGE[a]) + ends[j] * edge_b
                    blocks.append(r / (base + float(LAM_T[a])))
                parts.append(jnp.concatenate(blocks, axis=0))
            back = dot3(kxp, split(jnp.concatenate(parts, axis=1)))
            for i in range(2):
                o = 2 * q + i
                ybuf[:, 8 * o : 8 * o + 8, p * NZ : (p + 1) * NZ] = back[
                    :, i * NZ : (i + 1) * NZ
                ].reshape(H, 8, NZ)
    kyp = two(ky)
    copies = []
    for g in range(8):
        block = split(ybuf[4 * g : 4 * g + 4].reshape(4 * T, 2 * NZ))
        modal = split(dot3(kyp, block))
        res = dot3(modal, w)
        near = res[:, :NZ]
        far = res[:, NZ:]
        obuf[4 * g : 4 * g + 4] = (near + far).reshape(4, T, NZ)
        other = near - far
        for i in range(4):
            obuf[63 - 4 * g - i] = other[T * i : T * i + T]
        for i, lo in enumerate((4 * g, 60 - 4 * g)):
            copies.append(
                pltpu.make_async_copy(
                    obuf.at[lo : lo + 4], dest.at[lo : lo + 4], sems.at[2 * g + i]
                )
            )
            copies[-1].start()
    for copy in copies:
        copy.wait()


VMEM = pl.BlockSpec(memory_space=pltpu.VMEM)
HBM = pl.BlockSpec(memory_space=pltpu.HBM)
INTERPRET = False


def like(array):
    return jax.ShapeDtypeStruct(array.shape, array.dtype)


def shards(source, layer_mass, modes, mode_eigen):
    small, rowtab, ysel = tile_tables()
    tables = solve_tables()
    params = pltpu.CompilerParams(vmem_limit_bytes=40 * 1024 * 1024)
    eig = mode_eigen[None]
    mass = layer_mass[None]
    edge_shape = jax.ShapeDtypeStruct((NZ, 1, 2 * NZ), F32)
    kron = (2, 8 * H, 8 * H)
    made = pl.pallas_call(
        forward_kernel,
        out_shape=(
            jax.ShapeDtypeStruct((2, H, T, NZ), F32),
            edge_shape,
            jax.ShapeDtypeStruct(kron, BF16),
            jax.ShapeDtypeStruct((2, *kron), BF16),
            like(modes),
            like(eig),
            like(rowtab),
            *[like(t) for t in tables],
        ),
        in_specs=[HBM] * (7 + len(tables)),
        out_specs=[VMEM] * (7 + len(tables)),
        scratch_shapes=[
            pltpu.VMEM((T, T, NZ), F32),
            pltpu.VMEM((1, NZ), F32),
            pltpu.VMEM(small.shape, F32),
            pltpu.VMEM(ysel.shape, BF16),
            pltpu.VMEM((2, *kron), BF16),
            pltpu.VMEM((H, T, 2 * NZ), F32),
            pltpu.SemaphoreType.DMA((22 + len(tables),)),
        ],
        compiler_params=params,
        interpret=INTERPRET,
        name="forward",
    )(source, mass, modes, eig, small, rowtab, ysel, *tables)
    coef, edges, ky, kxt, modes, eig, rowtab = made[:7]
    edges = lax.all_to_all(edges, AXES, split_axis=0, concat_axis=0, tiled=True)
    values = pl.pallas_call(
        interface_kernel,
        out_shape=edge_shape,
        in_specs=[VMEM] * (2 + len(tables)),
        out_specs=VMEM,
        scratch_shapes=[pltpu.VMEM((NZ, NZ), F32)],
        compiler_params=params,
        interpret=INTERPRET,
        name="interface",
    )(edges, eig, *made[7:])
    values = lax.all_to_all(values, AXES, split_axis=0, concat_axis=0, tiled=True)
    return pl.pallas_call(
        backward_kernel,
        out_shape=jax.ShapeDtypeStruct((T, T, NZ), F32),
        in_specs=[VMEM] * 7,
        out_specs=HBM,
        scratch_shapes=[
            pltpu.VMEM((H, T, 2 * NZ), F32),
            pltpu.VMEM((2 * NZ, NZ), F32),
            pltpu.VMEM((T, T, NZ), F32),
            pltpu.SemaphoreType.DMA((16,)),
        ],
        compiler_params=params,
        interpret=INTERPRET,
        name="backward",
    )(coef, values, modes, eig, ky, kxt, rowtab)


def solution(mesh):
    placed = (P("px", "py", None), P(), P(), P())
    return jax.shard_map(
        shards, mesh=mesh, in_specs=placed, out_specs=P("px", "py", None), check_vma=False
    )
```

time: 62 us -> 70 us (1.13)
  local copies, waits for them, and re-layouts: 9.57 us -> 13.5 us
  Pallas kernels: 16.3 us -> 20.2 us
    pallas_call x1, Pallas kernels: 3.5 us -> 10.7 us  [shards(): pl.pallas_call(forward_kernel, out_shape=(jax.ShapeDtypeStruct((2, H, T,...]
    unnamed x34 -> x30, local copies, waits for them, and re-layouts: 8.78 us -> 13.5 us
    pallas_call x1, Pallas kernels: 8.19 us -> 5.31 us  [shards(): pl.pallas_call(interface_kernel, out_shape=edge_shape, in_specs=[VMEM] *...]
    broadcast_in_dim x1 -> x0, local copies, waits for them, and re-layouts: 0.79 us -> none  [shards(): layer_mass[:, None]]
where the time goes in v1:
time: 70 us; the launch traced here: 69.3 us
  blocking collectives  35.5 us (51%)
  Pallas kernels  20.2 us (29%)
  local copies, waits for them, and re-layouts  13.5 us (19%)
    all_to_all x1, blocking collectives, shards(): edges = lax.all_to_all(edges, AXES, split_axis=0, concat_axis=0, tiled=True)  21.3 us
    all_to_all x1, blocking collectives, shards(): lax.all_to_all(values, AXES, split_axis=0, concat_axis=0, tiled=True)  14.2 us
    unnamed x30, local copies, waits for them, and re-layouts  13.5 us
    pallas_call x1, Pallas kernels, shards(): pl.pallas_call(forward_kernel, out_shape=(jax.ShapeDtypeStruct((2, H, T,...  10.7 us
    pallas_call x1, Pallas kernels, shards(): pl.pallas_call(interface_kernel, out_shape=edge_shape, in_specs=[VMEM] *...  5.31 us
    pallas_call x1, Pallas kernels, shards(): pl.pallas_call(backward_kernel, out_shape=jax.ShapeDtypeStruct((T, T, NZ)...  4.16 us

profile of v1, /device:TPU:1, one launch (start us, length us, event | category | flops | bytes accessed | tf_op | source)
XLA Modules:
  0.0 69.3 jit_solution(6618316164320824450)
XLA Ops:
  0.0 0.0 copy-start
  0.0 1.6 %copy-done = f32[64,64,128]{2,1,0:T(8,128)S(1)} copy-done((f32[64,64,128]{2,1,0:T(8,128)S(1)}, f32[64,64,128]{2,1,0:T(8,128)}, u32[]{:S(2)}) %copy-start) | copy-done | bytes 2097176
  1.6 0.0 copy-start.1
  1.6 1.0 %copy-done.1 = bf16[1024,256]{1,0:T(8,128)(2,1)S(1)} copy-done((bf16[1024,256]{1,0:T(8,128)(2,1)S(1)}, bf16[1024,256]{1,0:T(8,128)(2,1)}, u32[]{:S(2)}) %copy-start.1) | copy-done | bytes 524312
  2.6 0.0 copy-start.2
  2.6 1.0 %copy-done.2 = bf16[2,2,256,256]{3,2,1,0:T(8,128)(2,1)S(1)} copy-done((bf16[2,2,256,256]{3,2,1,0:T(8,128)(2,1)S(1)}, bf16[2,2,256,256]{3,2,1,0:T(8,128)(2,1)}, u32[]{:S(2)}) %copy-start.2) | copy-done | bytes 524312
  3.7 0.0 copy-start.3
  3.7 0.9 %copy-done.3 = f32[4,128,128]{2,1,0:T(8,128)S(1)} copy-done((f32[4,128,128]{2,1,0:T(8,128)S(1)}, f32[4,128,128]{2,1,0:T(8,128)}, u32[]{:S(2)}) %copy-start.3) | copy-done | bytes 262168
  4.6 0.0 copy-start.4
  4.6 0.9 %copy-done.4 = bf16[2,128,512]{2,1,0:T(8,128)(2,1)S(1)} copy-done((bf16[2,128,512]{2,1,0:T(8,128)(2,1)S(1)}, bf16[2,128,512]{2,1,0:T(8,128)(2,1)}, u32[]{:S(2)}) %copy-start.4) | copy-done | bytes 262168
  5.6 0.0 copy-start.5
  5.6 0.9 %copy-done.5 = bf16[1024,128]{1,0:T(8,128)(2,1)S(1)} copy-done((bf16[1024,128]{1,0:T(8,128)(2,1)S(1)}, bf16[1024,128]{1,0:T(8,128)(2,1)}, u32[]{:S(2)}) %copy-start.5) | copy-done | bytes 262168
  6.5 0.0 copy-start.6
  6.5 0.9 %copy-done.6 = f32[192,256]{1,0:T(8,128)S(1)} copy-done((f32[192,256]{1,0:T(8,128)S(1)}, f32[192,256]{1,0:T(8,128)}, u32[]{:S(2)}) %copy-start.6) | copy-done | bytes 196632
  7.5 0.0 copy-start.7
  7.5 0.8 %copy-done.7 = f32[128,128]{1,0:T(8,128)S(1)} copy-done((f32[128,128]{1,0:T(8,128)S(1)}, f32[128,128]{1,0:T(8,128)}, u32[]{:S(2)}) %copy-start.7) | copy-done | bytes 65560
  8.3 0.0 copy-start.8
  8.3 0.8 %copy-done.8 = bf16[2,2,16,512]{3,2,1,0:T(8,128)(2,1)S(1)} copy-done((bf16[2,2,16,512]{3,2,1,0:T(8,128)(2,1)S(1)}, bf16[2,2,16,512]{3,2,1,0:T(8,128)(2,1)}, u32[]{:S(2)}) %copy-start.8) | copy-done | bytes 65560
  9.1 0.0 copy-start.9
  9.1 0.8 %copy-done.9 = f32[128,128]{1,0:T(8,128)S(1)} copy-done((f32[128,128]{1,0:T(8,128)S(1)}, f32[128,128]{1,0:T(8,128)}, u32[]{:S(2)}) %copy-start.9) | copy-done | bytes 65560
  10.0 0.0 copy-start.10
  10.0 0.8 %copy-done.10 = f32[32,256]{1,0:T(8,128)S(1)} copy-done((f32[32,256]{1,0:T(8,128)S(1)}, f32[32,256]{1,0:T(8,128)}, u32[]{:S(2)}) %copy-start.10) | copy-done | bytes 32792
  10.7 0.0 copy-start.11
  10.7 0.8 %copy-done.11 = bf16[64,256]{1,0:T(8,128)(2,1)S(1)} copy-done((bf16[64,256]{1,0:T(8,128)(2,1)S(1)}, bf16[64,256]{1,0:T(8,128)(2,1)}, u32[]{:S(2)}) %copy-start.11) | copy-done | bytes 32792
  11.5 0.0 copy-start.12
  11.5 0.7 copy-done.12
  12.2 0.0 copy-start.13
  12.2 0.7 copy-done.13
  12.8 0.0 copy-start.14
  12.8 0.7 copy-done.14
  13.5 10.7 %forward.1 = (f32[2,32,64,128]{3,2,1,0:T(8,128)S(1)}, f32[128,1,256]{2,1,0:T(1,128)S(1)}, bf16[2,256,256]{2,1,0:T(8,128)(2,1)S(1)}, bf16[2,2,256,256]{3,2,1,0:T(...) custom-call(f32[64,64,128]{2,1,0:T(8,128)S(1)} %copy-done, ...), custom_call_target="tpu_custom_call" | custom-call | tf_op jit(solution)/shard_map/forward/pallas_call | solution.py:413
  24.2 21.3 %all_to_all.10.got = f32[128,1,256]{2,1,0:T(1,128)S(1)} all-to-all(f32[128,1,256]{2,1,0:T(1,128)S(1)} %get-tuple-element.21), channel_id=1, replica_groups=mesh['px'=16,'py'=8] {'px','py'}, dimensions={0} | all-to-all | bytes 262144 | tf_op jit(solution)/shard_map/all_to_all | solution.py:441
  45.5 5.3 %interface.1 = f32[128,1,256]{2,1,0:T(1,128)S(1)} custom-call(f32[128,1,256]{2,1,0:T(1,128)S(1)} %all_to_all.10.got, f32[1,128]{1,0:T(1,128)S(1)} %get-tuple-element.22.eig, bf16[2,2,256,256]{3,2,1,0:T(8,128)(2,1)S(1)} %get-tuple-element.23.cyl, bf16[1024,256]{1,0:T(8,128)(2,1)S(1)} %get-tuple-element.24.m12, bf16[1024,128]{1,0:T(8,128)(2,1)S(1)} %get-tuple-element.25.bkx, ...), custom_call_target="tpu_custom_call" | custom-call | tf_op jit(solution)/shard_map/interface/pallas_call | solution.py:442
  50.8 14.2 %all_to_all.11.got = f32[128,1,256]{2,1,0:T(1,128)S(1)} all-to-all(f32[128,1,256]{2,1,0:T(1,128)S(1)} %interface.1), channel_id=1, replica_groups=mesh['px'=16,'py'=8] {'px','py'}, dimensions={0} | all-to-all | bytes 262144 | tf_op jit(solution)/shard_map/all_to_all | solution.py:452
  65.0 4.2 %backward.1 = f32[64,64,128]{2,1,0:T(8,128)} custom-call(f32[2,32,64,128]{3,2,1,0:T(8,128)S(1)} %get-tuple-element.20.coef, f32[128,1,256]{2,1,0:T(1,128)S(1)} %all_to_all.11.got, f32[128,128]{1,0:T(8,128)S(1)} %get-tuple-element.31.modes, f32[1,128]{1,0:T(1,128)S(1)} %get-tuple-element.22.eig, bf16[2,256,256]{2,1,0:T(8,128)(2,1)S(1)} %get-tuple-element.32.ky, ...), custom_call_target="tpu_custom_call" | custom-call | tf_op jit(solution)/shard_map/backward/pallas_call | solution.py:453
Async XLA Ops:
  0.0 1.6 %copy-start = (f32[64,64,128]{2,1,0:T(8,128)S(1)}, f32[64,64,128]{2,1,0:T(8,128)}, u32[]{:S(2)}) copy-start(f32[64,64,128]{2,1,0:T(8,128)} %refs_0_.1) | copy-start | bytes 6291460
  1.6 1.0 %copy-start.1 = (bf16[1024,256]{1,0:T(8,128)(2,1)S(1)}, bf16[1024,256]{1,0:T(8,128)(2,1)}, u32[]{:S(2)}) copy-start(bf16[1024,256]{1,0:T(8,128)(2,1)} %constant.26.clone.refs_8_) | copy-start | bytes 1572868
  2.6 1.0 %copy-start.2 = (bf16[2,2,256,256]{3,2,1,0:T(8,128)(2,1)S(1)}, bf16[2,2,256,256]{3,2,1,0:T(8,128)(2,1)}, u32[]{:S(2)}) copy-start(bf16[2,2,256,256]{3,2,1,0:T(8,128)(2,1)} %constant.25.clone.refs_7_) | copy-start | bytes 1572868
  3.7 0.9 %copy-start.3 = (f32[4,128,128]{2,1,0:T(8,128)S(1)}, f32[4,128,128]{2,1,0:T(8,128)}, u32[]{:S(2)}) copy-start(f32[4,128,128]{2,1,0:T(8,128)} %constant.31.clone.refs_13_) | copy-start | bytes 786436
  4.6 0.9 %copy-start.4 = (bf16[2,128,512]{2,1,0:T(8,128)(2,1)S(1)}, bf16[2,128,512]{2,1,0:T(8,128)(2,1)}, u32[]{:S(2)}) copy-start(bf16[2,128,512]{2,1,0:T(8,128)(2,1)} %constant.29.clone.refs_11_) | copy-start | bytes 786436
  5.6 0.9 %copy-start.5 = (bf16[1024,128]{1,0:T(8,128)(2,1)S(1)}, bf16[1024,128]{1,0:T(8,128)(2,1)}, u32[]{:S(2)}) copy-start(bf16[1024,128]{1,0:T(8,128)(2,1)} %constant.27.clone.refs_9_) | copy-start | bytes 786436
  6.5 0.9 %copy-start.6 = (f32[192,256]{1,0:T(8,128)S(1)}, f32[192,256]{1,0:T(8,128)}, u32[]{:S(2)}) copy-start(f32[192,256]{1,0:T(8,128)} %constant.22.clone.refs_4_) | copy-start | bytes 589828
  7.5 0.8 %copy-start.7 = (f32[128,128]{1,0:T(8,128)S(1)}, f32[128,128]{1,0:T(8,128)}, u32[]{:S(2)}) copy-start(f32[128,128]{1,0:T(8,128)} %refs_2_.1) | copy-start | bytes 196612
  8.3 0.8 %copy-start.8 = (bf16[2,2,16,512]{3,2,1,0:T(8,128)(2,1)S(1)}, bf16[2,2,16,512]{3,2,1,0:T(8,128)(2,1)}, u32[]{:S(2)}) copy-start(bf16[2,2,16,512]{3,2,1,0:T(8,128)(2,1)} %constant.28.clone.refs_10_) | copy-start | bytes 196612
  9.1 0.8 %copy-start.9 = (f32[128,128]{1,0:T(8,128)S(1)}, f32[128,128]{1,0:T(8,128)}, u32[]{:S(2)}) copy-start(f32[128,128]{1,0:T(8,128)} %constant.23.clone.refs_5_) | copy-start | bytes 196612
  10.0 0.8 %copy-start.10 = (f32[32,256]{1,0:T(8,128)S(1)}, f32[32,256]{1,0:T(8,128)}, u32[]{:S(2)}) copy-start(f32[32,256]{1,0:T(8,128)} %constant.30.clone.refs_12_) | copy-start | bytes 98308
  10.7 0.8 %copy-start.11 = (bf16[64,256]{1,0:T(8,128)(2,1)S(1)}, bf16[64,256]{1,0:T(8,128)(2,1)}, u32[]{:S(2)}) copy-start(bf16[64,256]{1,0:T(8,128)(2,1)} %constant.24.clone.refs_6_) | copy-start | bytes 98308
  11.5 0.7 copy-start.12
  12.2 0.7 copy-start.13
  12.8 0.7 copy-start.14

commit v2 on v1

--- a/solution.py
+++ b/solution.py
@@ -410,6 +410,10 @@
     mass = layer_mass[None]
     edge_shape = jax.ShapeDtypeStruct((NZ, 1, 2 * NZ), F32)
     kron = (2, 8 * H, 8 * H)
+    operands = [
+        pltpu.with_memory_space_constraint(jnp.asarray(v), pltpu.HBM)
+        for v in (source, mass, modes, eig, small, rowtab, ysel, *tables)
+    ]
     made = pl.pallas_call(
         forward_kernel,
         out_shape=(
@@ -436,7 +440,7 @@
         compiler_params=params,
         interpret=INTERPRET,
         name="forward",
-    )(source, mass, modes, eig, small, rowtab, ysel, *tables)
+    )(*operands)
     coef, edges, ky, kxt, modes, eig, rowtab = made[:7]
     edges = lax.all_to_all(edges, AXES, split_axis=0, concat_axis=0, tiled=True)
     values = pl.pallas_call(

time: 70 us -> 53.6 us (0.77)
  local copies, waits for them, and re-layouts: 13.5 us -> 0 us
  Pallas kernels: 20.2 us -> 17.8 us
    unnamed x30 -> x0, local copies, waits for them, and re-layouts: 13.5 us -> none
    pallas_call x1, Pallas kernels: 10.7 us -> 8.28 us  [shards(): pl.pallas_call(forward_kernel, out_shape=(jax.ShapeDtypeStruct((2, H, T,...]
where the time goes in v2:
time: 53.6 us; the launch traced here: 53.4 us
  blocking collectives  35.5 us (66%)
  Pallas kernels  17.8 us (33%)
    all_to_all x1, blocking collectives, shards(): edges = lax.all_to_all(edges, AXES, split_axis=0, concat_axis=0, tiled=True)  21.3 us
    all_to_all x1, blocking collectives, shards(): lax.all_to_all(values, AXES, split_axis=0, concat_axis=0, tiled=True)  14.2 us
    pallas_call x1, Pallas kernels, shards(): pl.pallas_call(forward_kernel, out_shape=(jax.ShapeDtypeStruct((2, H, T,...  8.28 us
    pallas_call x1, Pallas kernels, shards(): pl.pallas_call(interface_kernel, out_shape=edge_shape, in_specs=[VMEM] *...  5.33 us
    pallas_call x1, Pallas kernels, shards(): pl.pallas_call(backward_kernel, out_shape=jax.ShapeDtypeStruct((T, T, NZ)...  4.18 us

profile of v2, /device:TPU:1, one launch (start us, length us, event | category | flops | bytes accessed | tf_op | source)
XLA Modules:
  0.0 53.4 jit_solution(7690222075503926004)
XLA Ops:
  0.0 8.3 %forward.1 = (f32[2,32,64,128]{3,2,1,0:T(8,128)S(1)}, f32[128,1,256]{2,1,0:T(1,128)S(1)}, bf16[2,256,256]{2,1,0:T(8,128)(2,1)S(1)}, bf16[2,2,256,256]{3,2,1,0:T(...) custom-call(f32[64,64,128]{2,1,0:T(8,128)} %refs_0_.1, ...), custom_call_target="tpu_custom_call" | custom-call | tf_op jit(solution)/shard_map/forward/pallas_call | solution.py:417
  8.3 21.3 %all_to_all.10.got = f32[128,1,256]{2,1,0:T(1,128)S(1)} all-to-all(f32[128,1,256]{2,1,0:T(1,128)S(1)} %get-tuple-element.21), channel_id=1, replica_groups=mesh['px'=16,'py'=8] {'px','py'}, dimensions={0} | all-to-all | bytes 262144 | tf_op jit(solution)/shard_map/all_to_all | solution.py:445
  29.6 5.3 %interface.1 = f32[128,1,256]{2,1,0:T(1,128)S(1)} custom-call(f32[128,1,256]{2,1,0:T(1,128)S(1)} %all_to_all.10.got, f32[1,128]{1,0:T(1,128)S(1)} %get-tuple-element.22.eig, bf16[2,2,256,256]{3,2,1,0:T(8,128)(2,1)S(1)} %get-tuple-element.23.cyl, bf16[1024,256]{1,0:T(8,128)(2,1)S(1)} %get-tuple-element.24.m12, bf16[1024,128]{1,0:T(8,128)(2,1)S(1)} %get-tuple-element.25.bkx, ...), custom_call_target="tpu_custom_call" | custom-call | tf_op jit(solution)/shard_map/interface/pallas_call | solution.py:446
  34.9 14.2 %all_to_all.11.got = f32[128,1,256]{2,1,0:T(1,128)S(1)} all-to-all(f32[128,1,256]{2,1,0:T(1,128)S(1)} %interface.1), channel_id=1, replica_groups=mesh['px'=16,'py'=8] {'px','py'}, dimensions={0} | all-to-all | bytes 262144 | tf_op jit(solution)/shard_map/all_to_all | solution.py:456
  49.1 4.2 %backward.1 = f32[64,64,128]{2,1,0:T(8,128)} custom-call(f32[2,32,64,128]{3,2,1,0:T(8,128)S(1)} %get-tuple-element.20.coef, f32[128,1,256]{2,1,0:T(1,128)S(1)} %all_to_all.11.got, f32[128,128]{1,0:T(8,128)S(1)} %get-tuple-element.31.modes, f32[1,128]{1,0:T(1,128)S(1)} %get-tuple-element.22.eig, bf16[2,256,256]{2,1,0:T(8,128)(2,1)S(1)} %get-tuple-element.32.ky, ...), custom_call_target="tpu_custom_call" | custom-call | tf_op jit(solution)/shard_map/backward/pallas_call | solution.py:457

commit v3 on v2

--- a/solution.py
+++ b/solution.py
@@ -47,7 +47,7 @@
     small = np.concatenate([spread, np.tile(SINE, (1, 4))]).astype(np.float32)
     edge_b = np.broadcast_to(EDGE[:, None], (T, NZ))
     lam_b = np.broadcast_to(LAM_T[:, None], (T, NZ))
-    rowtab = np.concatenate([edge_b, lam_b]).astype(np.float32)
+    rowtab = np.concatenate([edge_b, lam_b], axis=1).astype(np.float32)
     signs = np.stack([np.ones(8), (-1.0) ** np.arange(8)])
     ysel = np.concatenate([np.kron(np.eye(H), signs[s : s + 1]) for s in range(2)])
     return small, rowtab, ysel.astype(jnp.bfloat16)
@@ -93,7 +93,20 @@
     tz = np.concatenate(tz).astype(np.float32)
     tr = np.stack(tr).astype(np.float32)
     lam_y = (2.0 - 2.0 * np.cos(np.pi * be / NY)).astype(np.float32)[None]
-    return cyl, m12, bkx_all, bkxt, pair(bys), tz, tr, lam_y
+    bys = pair(bys)
+    bys = np.concatenate([bys[:, :, :256], bys[:, :, 256:]], axis=1)
+    bkx_all = bkx_all.reshape(2, 2, 256, 128)
+    bkx_all = np.concatenate([bkx_all[:, 0], bkx_all[:, 1]], axis=2)
+    bkxt = bkxt.reshape(2, 2, 16, 2, 256).transpose(0, 1, 3, 2, 4)
+    tr = np.stack([np.concatenate([tr[2 * p], tr[2 * p + 1]], axis=1) for p in range(2)])
+    small, rowtab, ysel = tile_tables()
+    lam_y = np.concatenate([lam_y.reshape(2, 256), np.zeros((6, 256), np.float32)])
+    flat = lambda parts: np.concatenate([t.reshape(-1, 256) for t in parts])
+    return flat([small, rowtab, tz, tr, lam_y]), flat([cyl, m12, bkx_all, bys, bkxt, ysel])
+
+
+SMALL, ROWTAB, TZ, TR, LAM_Y = 0, 192, 256, 288, 544
+CYL, M12, BKX, BYS, BKXT, YSEL = 0, 1024, 2048, 2560, 3072, 3200
 
 
 def split(value):
@@ -128,54 +141,57 @@
     return lax.broadcasted_iota(jnp.int32, shape, axis)
 
 
-def forward_kernel(*refs):
-    src_in, mass_in, modes_in, eig_in, small_in, rowtab_in, ysel_in = refs[:7]
-    tables_in = refs[7:15]
-    coef, edges, ky, kxt, modes, eig, rowtab = refs[15:22]
-    tables = refs[22:30]
-    src, mass, small, ysel, kx, ybuf, sems = refs[30:]
-    jobs = [(small_in, small), (mass_in, mass), (modes_in, modes)]
-    for g in range(8):
-        for lo in (4 * g, 60 - 4 * g):
-            jobs.append((src_in.at[lo : lo + 4], src.at[lo : lo + 4]))
-    jobs += [(eig_in, eig), (rowtab_in, rowtab), (ysel_in, ysel)]
-    jobs += list(zip(tables_in, tables))
+def forward_kernel(
+    src_in, mass_in, modes_in, eig_in, tab_in, wide_in,
+    coef, recip, edges, ky, kxt, modes, eig, tab, wide,
+    src, mass, kx, ybuf, sems,
+):
+    jobs = [(tab_in, tab), (eig_in, eig), (mass_in, mass), (modes_in, modes)]
+    for lo, hi in ((0, 16), (48, 64), (16, 48)):
+        jobs.append((src_in.at[lo:hi], src.at[lo:hi]))
+    jobs.append((wide_in, wide))
     copies = [pltpu.make_async_copy(a, b, sems.at[i]) for i, (a, b) in enumerate(jobs)]
     for copy in copies:
         copy.start()
-    for copy in copies[:3]:
-        copy.wait()
+    copies[0].wait()
     row_block = lanes((T, 4 * T), 1) // T
     for i in range(4):
-        part = split(jnp.where(row_block == i, small[4 * H : 4 * H + T, :], 0.0))
+        part = split(jnp.where(row_block == i, tab[4 * H : 4 * H + T, :], 0.0))
         for h in range(2):
             ky[h, T * i : T * i + T, :] = part[h]
     diagonal = lanes((8, 8 * H), 1) % 8 == lanes((8, 8 * H), 0)
     for t in range(4):
-        spread = [
-            jnp.where(diagonal, small[H * t + j : H * t + j + 1, :], 0.0) for j in range(H)
-        ]
+        spread = [jnp.where(diagonal, tab[H * t + j : H * t + j + 1, :], 0.0) for j in range(H)]
         part = split(jnp.concatenate(spread, axis=0))
         for h in range(2):
             if t < 2:
                 kx[t, h] = part[h]
             else:
                 kxt[t - 2, h] = part[h]
+    copies[1].wait()
+    eig_row = eig[...]
+    for o in range(8):
+        base = eig_row + tab[ROWTAB + 8 * o : ROWTAB + 8 * o + 8, NZ : 2 * NZ]
+        for p in range(2):
+            for j in range(H):
+                recip[p, j, 8 * o : 8 * o + 8, :] = 1.0 / (base + float(LAM_T[2 * j + p]))
+    copies[2].wait()
+    copies[3].wait()
     mass_col = jnp.broadcast_to(mass[...], (NZ, NZ)).T
     w = split(mass_col * modes[...])
     w = block_diag2(w[0]), block_diag2(w[1])
     kyp = two(ky)
     for g in range(8):
-        for copy in copies[3 + 2 * g : 5 + 2 * g]:
-            copy.wait()
+        if g == 0:
+            copies[4].wait()
+            copies[5].wait()
+        if g == 4:
+            copies[6].wait()
         near = src[4 * g : 4 * g + 4].reshape(4 * T, NZ)
         far = jnp.concatenate([src[63 - 4 * g - i] for i in range(4)], axis=0)
         folded = split(jnp.concatenate([near + far, near - far], axis=1))
         modal = split(dot3(folded, w))
         ybuf[4 * g : 4 * g + 4] = dot3(kyp, modal).reshape(4, T, 2 * NZ)
-    for copy in copies[19:22]:
-        copy.wait()
-    eig_row = eig[...]
     across = [[None] * 8, [None] * 8]
     along = []
     for p in range(2):
@@ -191,31 +207,28 @@
                 o = 2 * q + i
                 block = spec[:, i * NZ : (i + 1) * NZ]
                 coef[p, :, 8 * o : 8 * o + 8, :] = block.reshape(H, 8, NZ)
-                base = eig_row + rowtab[T + 8 * o : T + 8 * o + 8, :]
-                edge_b = rowtab[8 * o : 8 * o + 8, :]
+                edge_b = tab[ROWTAB + 8 * o : ROWTAB + 8 * o + 8, 0:NZ]
                 acc_x = None
                 for j in range(H):
-                    a = 2 * j + p
-                    v = block[8 * j : 8 * j + 8] / (base + float(LAM_T[a]))
-                    vx = v * float(EDGE[a])
+                    v = block[8 * j : 8 * j + 8] * recip[p, j, 8 * o : 8 * o + 8, :]
+                    vx = v * float(EDGE[2 * j + p])
                     vy = v * edge_b
                     acc_x = vx if acc_x is None else acc_x + vx
                     acc_y[j] = vy if acc_y[j] is None else acc_y[j] + vy
                 across[p][o] = acc_x
         along.append(jnp.concatenate(acc_y, axis=0))
+    copies[7].wait()
     even = jnp.concatenate(across[0], axis=0)
     odd = jnp.concatenate(across[1], axis=0)
     sums = split(jnp.concatenate(along, axis=1))
-    sel = ysel[...]
+    sel = wide[YSEL : YSEL + T, :]
     ends = dot(sel, sums[0]) + dot(sel, sums[1])
     first = jnp.concatenate([ends[:H, :NZ], ends[:H, NZ:]], axis=0)
     last = jnp.concatenate([ends[H:, :NZ], ends[H:, NZ:]], axis=0)
     xs = jnp.concatenate([even + odd, even - odd], axis=0)
     ys = jnp.concatenate([first, last], axis=0)
-    edges[:, 0, 0:NZ] = xs.T
-    edges[:, 0, NZ : 2 * NZ] = ys.T
-    for copy in copies[22:]:
-        copy.wait()
+    edges[pl.ds(0, NZ, stride=2), :] = xs.T
+    edges[pl.ds(1, NZ, stride=2), :] = ys.T
 
 
 def turned(m):
@@ -226,7 +239,9 @@
     return pltpu.roll(m, T, 1)
 
 
-def interface_kernel(got, eig, cyl, m12, bkx, bkxt, bys, tz, tr, lam_y, out, xbuf):
+def interface_kernel(got, eig, tab, wide, out, xbuf):
+    block = lambda at: wide[at : at + 256, :]
+    cyl = [(block(CYL + 512 * i), block(CYL + 512 * i + 256)) for i in range(2)]
     mode = lax.axis_index("px") * PY + lax.axis_index("py")
     mu = jnp.sum(jnp.where(lanes((1, NZ), 1) == mode, eig[...], 0.0), axis=1, keepdims=True)
     lane = lanes((NZ, NZ), 1)
@@ -236,8 +251,8 @@
     low64 = low[:T]
     sign_b = jnp.where(lanes((2 * PX, NZ), 1) % 2 == 0, 1.0, -1.0)
     sign_a = jnp.where(lanes((T, NZ), 1) % T < H, 1.0, -1.0)
-    gx = got[:, 0, 0:NZ]
-    gy = got[:, 0, NZ : 2 * NZ]
+    gx = got[pl.ds(0, NZ, stride=2), :]
+    gy = got[pl.ds(1, NZ, stride=2), :]
 
     mirror = swap(turned(gx))
     xbuf[...] = jnp.where(low, gx + mirror, swap(gx - mirror))
@@ -253,7 +268,7 @@
     line_e = jnp.concatenate([tiles[q] + flipped[q] for q in range(2)], axis=1)
     line_o = jnp.concatenate([tiles[q] - flipped[q] for q in range(2)], axis=1)
     t1 = jnp.concatenate(
-        [dot3(split(line_e), two(cyl, 0)), dot3(split(line_o), two(cyl, 1))], axis=1
+        [dot3(split(line_e), cyl[0]), dot3(split(line_o), cyl[1])], axis=1
     )
     t1h, t1l = split(t1)
 
@@ -263,9 +278,13 @@
     ends = jnp.concatenate(
         [jnp.where(low64, part_e, swap(part_o)), jnp.where(low64, swap(part_e), part_o)], axis=0
     ).T
-    by_h, by_l = two(bys)
+    by_h, by_l = [
+        jnp.concatenate([wide[at : at + NZ, :], wide[at + NZ : at + 2 * NZ, :]], axis=1)
+        for at in (BYS, BYS + 256)
+    ]
     by_lh = jnp.concatenate([by_l, by_h], axis=0)
-    shift = lam_y[...] + mu
+    lam_y = jnp.concatenate([tab[LAM_Y : LAM_Y + 1, :], tab[LAM_Y + 1 : LAM_Y + 2, :]], axis=1)
+    shift = lam_y + mu
     back_x, back_y = [], []
     for p in range(2):
         e = split(ends[T * p : T * p + T])
@@ -276,32 +295,34 @@
         weights = jnp.concatenate([by_h, th, th, tl, pad], axis=0)
         sum_x = sum_y = None
         for c in range(2):
-            rows = slice(512 * p + 256 * c, 512 * p + 256 * c + 256)
-            m = m12[rows]
+            m = block(M12 + 512 * p + 256 * c)
             zz = dot(m, ehh) + dot(m[:, :NZ], el)
-            zz = (zz.reshape(16, 16, 256) * tz[16 * p : 16 * p + 16][None]).reshape(256, 256)
+            zz = (zz.reshape(16, 16, 256) * tab[TZ + 16 * p : TZ + 16 * p + 16, :][None]).reshape(256, 256)
             zh, zl = split(zz[:, :NZ] + zz[:, NZ:])
-            bk = bkx[rows]
+            bk = wide[BKX + 256 * p : BKX + 256 * p + 256, NZ * c : NZ * c + NZ]
             spec = dot(jnp.concatenate([zh, bk], axis=1), weights)
             spec += dot(jnp.concatenate([zh, zl], axis=1), by_lh)
             lams = bk[:, 48:51].astype(F32)
             lam = (lams[:, 2:3] + lams[:, 1:2]) + lams[:, 0:1]
             u = split(spec / (shift + lam))
-            cols = slice(256 * c, 256 * c + 256)
-            bx = dot3((bkxt[p, 0, :, cols], bkxt[p, 1, :, cols]), u)
+            at = [BKXT + 64 * p + 32 * h + 16 * c for h in range(2)]
+            bx = dot3((wide[at[0] : at[0] + 16, :], wide[at[1] : at[1] + 16, :]), u)
             r = dot3((by_h, by_l), u, NT)
-            turns = [jnp.concatenate([tr[2 * p + i]] * 2, axis=1) for i in range(2)]
+            turns = [
+                jnp.concatenate([tab[TR + NZ * p : TR + NZ * p + NZ, NZ * i : NZ * i + NZ]] * 2, axis=1)
+                for i in range(2)
+            ]
             rh, rl = split(jnp.concatenate([r * turns[0], r * turns[1]], axis=0))
-            wide = dot(rh, m)
-            by = wide[:, :NZ] + wide[:, NZ:] + dot(rl, m[:, :NZ])
+            both = dot(rh, m)
+            by = both[:, :NZ] + both[:, NZ:] + dot(rl, m[:, :NZ])
             sum_x = bx if c == 0 else sum_x + bx
             sum_y = by if c == 0 else sum_y + by
         back_x.append(sum_x)
         back_y.append(sum_y[:NZ] + swap(sum_y[NZ:]))
 
     bx = jnp.concatenate(back_x, axis=0)
-    we = dot3(split(bx[:, : NY // 2]), two(cyl, 0), NT)
-    wo = dot3(split(bx[:, NY // 2 :]), two(cyl, 1), NT)
+    we = dot3(split(bx[:, : NY // 2]), cyl[0], NT)
+    wo = dot3(split(bx[:, NY // 2 :]), cyl[1], NT)
     near = we + wo
     far = we - wo
     for q in range(4):
@@ -320,7 +341,7 @@
         jnp.concatenate([gx[:PY], other[:-PY]], axis=0),
         jnp.concatenate([other[PY:], gx[-PY:]], axis=0),
     )
-    out[:, 0, 0:NZ] = jnp.where(low, w, turned(w)) + own
+    out[pl.ds(0, NZ, stride=2), :] = jnp.where(low, w, turned(w)) + own
 
     near = back_y[0] + back_y[1]
     far = back_y[0] - back_y[1]
@@ -334,13 +355,12 @@
         jnp.where(row == 0, gy, pltpu.roll(other, 1, 0)),
         jnp.where(row == PY - 1, gy, pltpu.roll(other, NZ - 1, 0)),
     )
-    out[:, 0, NZ : 2 * NZ] = w + own
-
-
-def backward_kernel(coef, got, modes, eig, ky, kxt, rowtab, dest, ybuf, qbuf, obuf, sems):
-    qbuf[0:NZ] = got[:, 0, 0:NZ].T
-    qbuf[NZ : 2 * NZ] = got[:, 0, NZ : 2 * NZ].T
-    eig_row = eig[...]
+    out[pl.ds(1, NZ, stride=2), :] = w + own
+
+
+def backward_kernel(coef, recip, got, modes, ky, kxt, tab, dest, ybuf, qbuf, obuf, sems):
+    qbuf[0:NZ] = got[pl.ds(0, NZ, stride=2), :].T
+    qbuf[NZ : 2 * NZ] = got[pl.ds(1, NZ, stride=2), :].T
     sign = jnp.where(lanes((8, NZ), 0) % 2 == 0, 1.0, -1.0)
     w = split(modes[...].T)
     w = block_diag2(w[0]), block_diag2(w[1])
@@ -356,13 +376,12 @@
                 near = qbuf[8 * o : 8 * o + 8]
                 far = qbuf[T + 8 * o : T + 8 * o + 8]
                 line = near + far if p == 0 else near - far
-                base = eig_row + rowtab[T + 8 * o : T + 8 * o + 8, :]
-                edge_b = rowtab[8 * o : 8 * o + 8, :]
+                edge_b = tab[ROWTAB + 8 * o : ROWTAB + 8 * o + 8, 0:NZ]
                 blocks = []
                 for j in range(H):
-                    a = 2 * j + p
-                    r = coef[p, j, 8 * o : 8 * o + 8, :] + line * float(EDGE[a]) + ends[j] * edge_b
-                    blocks.append(r / (base + float(LAM_T[a])))
+                    edge = line * float(EDGE[2 * j + p]) + ends[j] * edge_b
+                    r = coef[p, j, 8 * o : 8 * o + 8, :] + edge
+                    blocks.append(r * recip[p, j, 8 * o : 8 * o + 8, :])
                 parts.append(jnp.concatenate(blocks, axis=0))
             back = dot3(kxp, split(jnp.concatenate(parts, axis=1)))
             for i in range(2):
@@ -382,17 +401,15 @@
         other = near - far
         for i in range(4):
             obuf[63 - 4 * g - i] = other[T * i : T * i + T]
-        for i, lo in enumerate((4 * g, 60 - 4 * g)):
-            copies.append(
-                pltpu.make_async_copy(
-                    obuf.at[lo : lo + 4], dest.at[lo : lo + 4], sems.at[2 * g + i]
-                )
-            )
-            copies[-1].start()
+        for lo, hi in SENDS.get(g, ()):
+            i = len(copies)
+            copies.append(pltpu.make_async_copy(obuf.at[lo:hi], dest.at[lo:hi], sems.at[i]))
+            copies[i].start()
     for copy in copies:
         copy.wait()
 
 
+SENDS = {3: ((0, 16), (48, 64)), 5: ((16, 24), (40, 48)), 7: ((24, 40),)}
 VMEM = pl.BlockSpec(memory_space=pltpu.VMEM)
 HBM = pl.BlockSpec(memory_space=pltpu.HBM)
 INTERPRET = False
@@ -402,58 +419,60 @@
     return jax.ShapeDtypeStruct(array.shape, array.dtype)
 
 
+def exchange(value):
+    value = value.reshape(NZ, 1, 2 * NZ)
+    value = lax.all_to_all(value, AXES, split_axis=0, concat_axis=0, tiled=True)
+    return value.reshape(2 * NZ, NZ)
+
+
 def shards(source, layer_mass, modes, mode_eigen):
-    small, rowtab, ysel = tile_tables()
-    tables = solve_tables()
+    tab, wide = solve_tables()
     params = pltpu.CompilerParams(vmem_limit_bytes=40 * 1024 * 1024)
     eig = mode_eigen[None]
     mass = layer_mass[None]
-    edge_shape = jax.ShapeDtypeStruct((NZ, 1, 2 * NZ), F32)
+    edge_shape = jax.ShapeDtypeStruct((2 * NZ, NZ), F32)
+    field = jax.ShapeDtypeStruct((2, H, T, NZ), F32)
     kron = (2, 8 * H, 8 * H)
     operands = [
         pltpu.with_memory_space_constraint(jnp.asarray(v), pltpu.HBM)
-        for v in (source, mass, modes, eig, small, rowtab, ysel, *tables)
+        for v in (source, mass, modes, eig, tab, wide)
     ]
-    made = pl.pallas_call(
+    coef, recip, edges, ky, kxt, modes, eig, tab, wide = pl.pallas_call(
         forward_kernel,
         out_shape=(
-            jax.ShapeDtypeStruct((2, H, T, NZ), F32),
+            field,
+            field,
             edge_shape,
             jax.ShapeDtypeStruct(kron, BF16),
             jax.ShapeDtypeStruct((2, *kron), BF16),
             like(modes),
             like(eig),
-            like(rowtab),
-            *[like(t) for t in tables],
+            like(tab),
+            like(wide),
         ),
-        in_specs=[HBM] * (7 + len(tables)),
-        out_specs=[VMEM] * (7 + len(tables)),
+        in_specs=[HBM] * 6,
+        out_specs=[VMEM] * 9,
         scratch_shapes=[
             pltpu.VMEM((T, T, NZ), F32),
             pltpu.VMEM((1, NZ), F32),
-            pltpu.VMEM(small.shape, F32),
-            pltpu.VMEM(ysel.shape, BF16),
             pltpu.VMEM((2, *kron), BF16),
             pltpu.VMEM((H, T, 2 * NZ), F32),
-            pltpu.SemaphoreType.DMA((22 + len(tables),)),
+            pltpu.SemaphoreType.DMA((8,)),
         ],
         compiler_params=params,
         interpret=INTERPRET,
         name="forward",
     )(*operands)
-    coef, edges, ky, kxt, modes, eig, rowtab = made[:7]
-    edges = lax.all_to_all(edges, AXES, split_axis=0, concat_axis=0, tiled=True)
     values = pl.pallas_call(
         interface_kernel,
         out_shape=edge_shape,
-        in_specs=[VMEM] * (2 + len(tables)),
+        in_specs=[VMEM] * 4,
         out_specs=VMEM,
         scratch_shapes=[pltpu.VMEM((NZ, NZ), F32)],
         compiler_params=params,
         interpret=INTERPRET,
         name="interface",
-    )(edges, eig, *made[7:])
-    values = lax.all_to_all(values, AXES, split_axis=0, concat_axis=0, tiled=True)
+    )(exchange(edges), eig, tab, wide)
     return pl.pallas_call(
         backward_kernel,
         out_shape=jax.ShapeDtypeStruct((T, T, NZ), F32),
@@ -463,12 +482,12 @@
             pltpu.VMEM((H, T, 2 * NZ), F32),
             pltpu.VMEM((2 * NZ, NZ), F32),
             pltpu.VMEM((T, T, NZ), F32),
-            pltpu.SemaphoreType.DMA((16,)),
+            pltpu.SemaphoreType.DMA((5,)),
         ],
         compiler_params=params,
         interpret=INTERPRET,
         name="backward",
-    )(coef, values, modes, eig, ky, kxt, rowtab)
+    )(coef, recip, exchange(values), modes, ky, kxt, tab)
 
 
 def solution(mesh):

time: 53.6 us -> 50.6 us (0.944)
  Pallas kernels: 17.8 us -> 15 us
    pallas_call x1, Pallas kernels: 8.28 us -> 5.59 us  [shards(): pl.pallas_call(forward_kernel, out_shape=(field, field, edge_shape, jax.S...]
where the time goes in v3:
time: 50.6 us; the launch traced here: 50.5 us
  blocking collectives  35.5 us (70%)
  Pallas kernels  15 us (30%)
    all_to_all x2, blocking collectives, exchange(): value = lax.all_to_all(value, AXES, split_axis=0, concat_axis=0, tiled=True)  35.5 us
    pallas_call x1, Pallas kernels, shards(): pl.pallas_call(forward_kernel, out_shape=(field, field, edge_shape, jax.S...  5.59 us
    pallas_call x1, Pallas kernels, shards(): pl.pallas_call(interface_kernel, out_shape=edge_shape, in_specs=[VMEM] *...  5.27 us
    pallas_call x1, Pallas kernels, shards(): pl.pallas_call(backward_kernel, out_shape=jax.ShapeDtypeStruct((T, T, NZ)...  4.13 us

profile of v3, /device:TPU:1, one launch (start us, length us, event | category | flops | bytes accessed | tf_op | source)
XLA Modules:
  0.0 50.5 jit_solution(13599286564337410128)
XLA Ops:
  0.0 5.6 %forward.1 = (f32[2,32,64,128]{3,2,1,0:T(8,128)S(1)}, f32[2,32,64,128]{3,2,1,0:T(8,128)S(1)}, f32[256,128]{1,0:T(8,128)S(1)}, bf16[2,256,256]{2,1,0:T(8,128)(2,1...) custom-call(f32[64,64,128]{2,1,0:T(8,128)} %src_in.1, ...), custom_call_target="tpu_custom_call" | custom-call | tf_op jit(solution)/shard_map/forward/pallas_call | solution.py:440
  5.6 21.3 %all_to_all.10 = f32[128,1,256]{2,1,0:T(1,128)S(1)} all-to-all(f32[128,1,256]{2,1,0:T(1,128)S(1)} %bitcast.9), channel_id=1, replica_groups=mesh['px'=16,'py'=8] {'px','py'}, dimensions={0} | all-to-all | bytes 262144 | tf_op jit(solution)/shard_map/all_to_all | solution.py:424
  26.9 5.3 %interface.1 = f32[256,128]{1,0:T(8,128)S(1)} custom-call(f32[256,128]{1,0:T(8,128)S(1)} %bitcast.7, f32[1,128]{1,0:T(1,128)S(1)} %get-tuple-element.17.eig, f32[552,256]{1,0:T(8,128)S(1)} %get-tuple-element.18.tab, bf16[3264,256]{1,0:T(8,128)(2,1)S(1)} %get-tuple-element.19.wide), custom_call_target="tpu_custom_call" | custom-call | tf_op jit(solution)/shard_map/interface/pallas_call | solution.py:466
  32.2 14.2 %all_to_all.11 = f32[128,1,256]{2,1,0:T(1,128)S(1)} all-to-all(f32[128,1,256]{2,1,0:T(1,128)S(1)} %bitcast.8), channel_id=1, replica_groups=mesh['px'=16,'py'=8] {'px','py'}, dimensions={0} | all-to-all | bytes 262144 | tf_op jit(solution)/shard_map/all_to_all | solution.py:424
  46.3 4.1 %backward.1 = f32[64,64,128]{2,1,0:T(8,128)} custom-call(f32[2,32,64,128]{3,2,1,0:T(8,128)S(1)} %get-tuple-element.14.coef, f32[2,32,64,128]{3,2,1,0:T(8,128)S(1)} %get-tuple-element.15.recip, f32[256,128]{1,0:T(8,128)S(1)} %bitcast.6, f32[128,128]{1,0:T(8,128)S(1)} %get-tuple-element.20.modes, bf16[2,256,256]{2,1,0:T(8,128)(2,1)S(1)} %get-tuple-element.21.ky, ...), custom_call_target="tpu_custom_call" | custom-call | tf_op jit(solution)/shard_map/backward/pallas_call | solution.py:476

commit v4 on v3

--- a/solution.py
+++ b/solution.py
@@ -285,40 +285,50 @@
     by_lh = jnp.concatenate([by_l, by_h], axis=0)
     lam_y = jnp.concatenate([tab[LAM_Y : LAM_Y + 1, :], tab[LAM_Y + 1 : LAM_Y + 2, :]], axis=1)
     shift = lam_y + mu
-    back_x, back_y = [], []
+    chunks = [(p, c) for p in range(2) for c in range(2)]
+    m = [block(M12 + 512 * p + 256 * c) for p, c in chunks]
+    starts = []
+    weights = []
+    pad = jnp.zeros((NZ - 3 * PX, NY), BF16)
     for p in range(2):
         e = split(ends[T * p : T * p + T])
         eh, el = block_diag2(e[0]), block_diag2(e[1])
-        ehh = jnp.concatenate([eh, eh], axis=0)
+        starts.append((jnp.concatenate([eh, eh], axis=0), el))
         th, tl = t1h[PX * p : PX * p + PX], t1l[PX * p : PX * p + PX]
-        pad = jnp.zeros((NZ - 3 * PX, NY), BF16)
-        weights = jnp.concatenate([by_h, th, th, tl, pad], axis=0)
-        sum_x = sum_y = None
-        for c in range(2):
-            m = block(M12 + 512 * p + 256 * c)
-            zz = dot(m, ehh) + dot(m[:, :NZ], el)
-            zz = (zz.reshape(16, 16, 256) * tab[TZ + 16 * p : TZ + 16 * p + 16, :][None]).reshape(256, 256)
-            zh, zl = split(zz[:, :NZ] + zz[:, NZ:])
-            bk = wide[BKX + 256 * p : BKX + 256 * p + 256, NZ * c : NZ * c + NZ]
-            spec = dot(jnp.concatenate([zh, bk], axis=1), weights)
-            spec += dot(jnp.concatenate([zh, zl], axis=1), by_lh)
-            lams = bk[:, 48:51].astype(F32)
-            lam = (lams[:, 2:3] + lams[:, 1:2]) + lams[:, 0:1]
-            u = split(spec / (shift + lam))
-            at = [BKXT + 64 * p + 32 * h + 16 * c for h in range(2)]
-            bx = dot3((wide[at[0] : at[0] + 16, :], wide[at[1] : at[1] + 16, :]), u)
-            r = dot3((by_h, by_l), u, NT)
-            turns = [
-                jnp.concatenate([tab[TR + NZ * p : TR + NZ * p + NZ, NZ * i : NZ * i + NZ]] * 2, axis=1)
-                for i in range(2)
-            ]
-            rh, rl = split(jnp.concatenate([r * turns[0], r * turns[1]], axis=0))
-            both = dot(rh, m)
-            by = both[:, :NZ] + both[:, NZ:] + dot(rl, m[:, :NZ])
-            sum_x = bx if c == 0 else sum_x + bx
-            sum_y = by if c == 0 else sum_y + by
-        back_x.append(sum_x)
-        back_y.append(sum_y[:NZ] + swap(sum_y[NZ:]))
+        weights.append(jnp.concatenate([by_h, th, th, tl, pad], axis=0))
+    zs = []
+    for i, (p, c) in enumerate(chunks):
+        zz = dot(m[i], starts[p][0]) + dot(m[i][:, :NZ], starts[p][1])
+        turn = tab[TZ + 16 * p : TZ + 16 * p + 16, :][None]
+        zz = (zz.reshape(16, 16, 256) * turn).reshape(256, 256)
+        zs.append(split(zz[:, :NZ] + zz[:, NZ:]))
+    us = []
+    for i, (p, c) in enumerate(chunks):
+        zh, zl = zs[i]
+        bk = wide[BKX + 256 * p : BKX + 256 * p + 256, NZ * c : NZ * c + NZ]
+        spec = dot(jnp.concatenate([zh, bk], axis=1), weights[p])
+        spec += dot(jnp.concatenate([zh, zl], axis=1), by_lh)
+        lams = bk[:, 48:51].astype(F32)
+        lam = (lams[:, 2:3] + lams[:, 1:2]) + lams[:, 0:1]
+        us.append(split(spec / (shift + lam)))
+    bxs, rs = [], []
+    for i, (p, c) in enumerate(chunks):
+        r = dot3((by_h, by_l), us[i], NT)
+        turns = [
+            jnp.concatenate([tab[TR + NZ * p : TR + NZ * p + NZ, NZ * j : NZ * j + NZ]] * 2, axis=1)
+            for j in range(2)
+        ]
+        rs.append(split(jnp.concatenate([r * turns[0], r * turns[1]], axis=0)))
+        at = [BKXT + 64 * p + 32 * h + 16 * c for h in range(2)]
+        bxs.append(dot3((wide[at[0] : at[0] + 16, :], wide[at[1] : at[1] + 16, :]), us[i]))
+    bys = []
+    for i in range(4):
+        rh, rl = rs[i]
+        both = dot(rh, m[i])
+        bys.append(both[:, :NZ] + both[:, NZ:] + dot(rl, m[i][:, :NZ]))
+    back_x = [bxs[0] + bxs[1], bxs[2] + bxs[3]]
+    back_y = [bys[0] + bys[1], bys[2] + bys[3]]
+    back_y = [y[:NZ] + swap(y[NZ:]) for y in back_y]
 
     bx = jnp.concatenate(back_x, axis=0)
     we = dot3(split(bx[:, : NY // 2]), cyl[0], NT)

time: 50.6 us -> 48.8 us (0.964)
  Pallas kernels: 15 us -> 13.2 us
    pallas_call x1, Pallas kernels: 5.27 us -> 3.46 us  [shards(): pl.pallas_call(interface_kernel, out_shape=edge_shape, in_specs=[VMEM] *...]
where the time goes in v4:
time: 48.8 us; the launch traced here: 48.6 us
  blocking collectives  35.5 us (73%)
  Pallas kernels  13.2 us (27%)
    all_to_all x2, blocking collectives, exchange(): value = lax.all_to_all(value, AXES, split_axis=0, concat_axis=0, tiled=True)  35.5 us
    pallas_call x1, Pallas kernels, shards(): pl.pallas_call(forward_kernel, out_shape=(field, field, edge_shape, jax.S...  5.59 us
    pallas_call x1, Pallas kernels, shards(): pl.pallas_call(backward_kernel, out_shape=jax.ShapeDtypeStruct((T, T, NZ)...  4.13 us
    pallas_call x1, Pallas kernels, shards(): pl.pallas_call(interface_kernel, out_shape=edge_shape, in_specs=[VMEM] *...  3.46 us

profile of v4, /device:TPU:1, one launch (start us, length us, event | category | flops | bytes accessed | tf_op | source)
XLA Modules:
  0.0 48.6 jit_solution(3336153123581551819)
XLA Ops:
  0.0 5.6 %forward.1 = (f32[2,32,64,128]{3,2,1,0:T(8,128)S(1)}, f32[2,32,64,128]{3,2,1,0:T(8,128)S(1)}, f32[256,128]{1,0:T(8,128)S(1)}, bf16[2,256,256]{2,1,0:T(8,128)(2,1...) custom-call(f32[64,64,128]{2,1,0:T(8,128)} %src_in.1, ...), custom_call_target="tpu_custom_call" | custom-call | tf_op jit(solution)/shard_map/forward/pallas_call | solution.py:450
  5.6 21.3 %all_to_all.10 = f32[128,1,256]{2,1,0:T(1,128)S(1)} all-to-all(f32[128,1,256]{2,1,0:T(1,128)S(1)} %bitcast.9), channel_id=1, replica_groups=mesh['px'=16,'py'=8] {'px','py'}, dimensions={0} | all-to-all | bytes 262144 | tf_op jit(solution)/shard_map/all_to_all | solution.py:434
  26.9 3.5 %interface.1 = f32[256,128]{1,0:T(8,128)S(1)} custom-call(f32[256,128]{1,0:T(8,128)S(1)} %bitcast.7, f32[1,128]{1,0:T(1,128)S(1)} %get-tuple-element.17.eig, f32[552,256]{1,0:T(8,128)S(1)} %get-tuple-element.18.tab, bf16[3264,256]{1,0:T(8,128)(2,1)S(1)} %get-tuple-element.19.wide), custom_call_target="tpu_custom_call" | custom-call | tf_op jit(solution)/shard_map/interface/pallas_call | solution.py:476
  30.3 14.2 %all_to_all.11 = f32[128,1,256]{2,1,0:T(1,128)S(1)} all-to-all(f32[128,1,256]{2,1,0:T(1,128)S(1)} %bitcast.8), channel_id=1, replica_groups=mesh['px'=16,'py'=8] {'px','py'}, dimensions={0} | all-to-all | bytes 262144 | tf_op jit(solution)/shard_map/all_to_all | solution.py:434
  44.5 4.1 %backward.1 = f32[64,64,128]{2,1,0:T(8,128)} custom-call(f32[2,32,64,128]{3,2,1,0:T(8,128)S(1)} %get-tuple-element.14.coef, f32[2,32,64,128]{3,2,1,0:T(8,128)S(1)} %get-tuple-element.15.recip, f32[256,128]{1,0:T(8,128)S(1)} %bitcast.6, f32[128,128]{1,0:T(8,128)S(1)} %get-tuple-element.20.modes, bf16[2,256,256]{2,1,0:T(8,128)(2,1)S(1)} %get-tuple-element.21.ky, ...), custom_call_target="tpu_custom_call" | custom-call | tf_op jit(solution)/shard_map/backward/pallas_call | solution.py:486

commit v5 on v4

--- a/solution.py
+++ b/solution.py
@@ -126,6 +126,27 @@
     return dot(a[0], b[0], dims) + dot(a[0], b[1], dims) + dot(a[1], b[0], dims)
 
 
+def halves(value, axis):
+    size = value.shape[axis] // 2
+    if axis == 0:
+        return value[:size] + value[size:]
+    return value[:, :size] + value[:, size:]
+
+
+def vertical(rows, w):
+    return halves(dot(jnp.concatenate(split(rows), axis=1), w), 1)
+
+
+def vertical_table(w):
+    both = jnp.concatenate(split(w), axis=1)
+    return jnp.concatenate([both, both], axis=0)
+
+
+def along_y(table, block):
+    both = jnp.concatenate([block[: 2 * T], block[2 * T :]], axis=1)
+    return halves(dot(table, jnp.concatenate(split(both), axis=0)), 0)
+
+
 def block_diag2(w):
     zero = jnp.zeros_like(w)
     top = jnp.concatenate([w, zero], axis=1)
@@ -146,19 +167,17 @@
     coef, recip, edges, ky, kxt, modes, eig, tab, wide,
     src, mass, kx, ybuf, sems,
 ):
-    jobs = [(tab_in, tab), (eig_in, eig), (mass_in, mass), (modes_in, modes)]
-    for lo, hi in ((0, 16), (48, 64), (16, 48)):
-        jobs.append((src_in.at[lo:hi], src.at[lo:hi]))
-    jobs.append((wide_in, wide))
+    jobs = [(tab_in.at[:TZ], tab.at[:TZ]), (eig_in, eig), (mass_in, mass), (modes_in, modes)]
+    jobs += [(src_in, src), (wide_in, wide), (tab_in.at[TZ:], tab.at[TZ:])]
     copies = [pltpu.make_async_copy(a, b, sems.at[i]) for i, (a, b) in enumerate(jobs)]
     for copy in copies:
         copy.start()
     copies[0].wait()
-    row_block = lanes((T, 4 * T), 1) // T
-    for i in range(4):
+    row_block = lanes((T, 4 * T), 1) // T % 2
+    for i in range(2):
         part = split(jnp.where(row_block == i, tab[4 * H : 4 * H + T, :], 0.0))
         for h in range(2):
-            ky[h, T * i : T * i + T, :] = part[h]
+            ky[2 * T * h + T * i : 2 * T * h + T * i + T, :] = part[h]
     diagonal = lanes((8, 8 * H), 1) % 8 == lanes((8, 8 * H), 0)
     for t in range(4):
         spread = [jnp.where(diagonal, tab[H * t + j : H * t + j + 1, :], 0.0) for j in range(H)]
@@ -178,20 +197,21 @@
     copies[2].wait()
     copies[3].wait()
     mass_col = jnp.broadcast_to(mass[...], (NZ, NZ)).T
-    w = split(mass_col * modes[...])
-    w = block_diag2(w[0]), block_diag2(w[1])
-    kyp = two(ky)
+    w = vertical_table(mass_col * modes[...])
+    copies[4].wait()
+    mods = [[], []]
     for g in range(8):
-        if g == 0:
-            copies[4].wait()
-            copies[5].wait()
-        if g == 4:
-            copies[6].wait()
         near = src[4 * g : 4 * g + 4].reshape(4 * T, NZ)
         far = jnp.concatenate([src[63 - 4 * g - i] for i in range(4)], axis=0)
-        folded = split(jnp.concatenate([near + far, near - far], axis=1))
-        modal = split(dot3(folded, w))
-        ybuf[4 * g : 4 * g + 4] = dot3(kyp, modal).reshape(4, T, 2 * NZ)
+        mods[0].append(vertical(near + far, w))
+        mods[1].append(vertical(near - far, w))
+    table = ky[...]
+    for p in range(2):
+        for g in range(8):
+            res = along_y(table, mods[p][g])
+            for i in range(2):
+                part = res[:, i * NZ : i * NZ + NZ].reshape(2, T, NZ)
+                ybuf[4 * g + 2 * i : 4 * g + 2 * i + 2, :, p * NZ : p * NZ + NZ] = part
     across = [[None] * 8, [None] * 8]
     along = []
     for p in range(2):
@@ -217,7 +237,8 @@
                     acc_y[j] = vy if acc_y[j] is None else acc_y[j] + vy
                 across[p][o] = acc_x
         along.append(jnp.concatenate(acc_y, axis=0))
-    copies[7].wait()
+    copies[5].wait()
+    copies[6].wait()
     even = jnp.concatenate(across[0], axis=0)
     odd = jnp.concatenate(across[1], axis=0)
     sums = split(jnp.concatenate(along, axis=1))
@@ -283,6 +304,7 @@
         for at in (BYS, BYS + 256)
     ]
     by_lh = jnp.concatenate([by_l, by_h], axis=0)
+    by_hl = jnp.concatenate([by_h, by_l], axis=0)
     lam_y = jnp.concatenate([tab[LAM_Y : LAM_Y + 1, :], tab[LAM_Y + 1 : LAM_Y + 2, :]], axis=1)
     shift = lam_y + mu
     chunks = [(p, c) for p in range(2) for c in range(2)]
@@ -302,25 +324,32 @@
         turn = tab[TZ + 16 * p : TZ + 16 * p + 16, :][None]
         zz = (zz.reshape(16, 16, 256) * turn).reshape(256, 256)
         zs.append(split(zz[:, :NZ] + zz[:, NZ:]))
-    us = []
-    for i, (p, c) in enumerate(chunks):
-        zh, zl = zs[i]
-        bk = wide[BKX + 256 * p : BKX + 256 * p + 256, NZ * c : NZ * c + NZ]
-        spec = dot(jnp.concatenate([zh, bk], axis=1), weights[p])
-        spec += dot(jnp.concatenate([zh, zl], axis=1), by_lh)
-        lams = bk[:, 48:51].astype(F32)
-        lam = (lams[:, 2:3] + lams[:, 1:2]) + lams[:, 0:1]
-        us.append(split(spec / (shift + lam)))
-    bxs, rs = [], []
-    for i, (p, c) in enumerate(chunks):
-        r = dot3((by_h, by_l), us[i], NT)
-        turns = [
+    us, bxs, rs = [], [], []
+    turns = [
+        [
             jnp.concatenate([tab[TR + NZ * p : TR + NZ * p + NZ, NZ * j : NZ * j + NZ]] * 2, axis=1)
             for j in range(2)
         ]
-        rs.append(split(jnp.concatenate([r * turns[0], r * turns[1]], axis=0)))
-        at = [BKXT + 64 * p + 32 * h + 16 * c for h in range(2)]
-        bxs.append(dot3((wide[at[0] : at[0] + 16, :], wide[at[1] : at[1] + 16, :]), us[i]))
+        for p in range(2)
+    ]
+    for step in range(5):
+        if step < 4:
+            p, c = chunks[step]
+            zh, zl = zs[step]
+            bk = wide[BKX + 256 * p : BKX + 256 * p + 256, NZ * c : NZ * c + NZ]
+            spec = dot(jnp.concatenate([zh, bk], axis=1), weights[p])
+            spec += dot(jnp.concatenate([zh, zl], axis=1), by_lh)
+            lams = bk[:, 48:51].astype(F32)
+            lam = (lams[:, 2:3] + lams[:, 1:2]) + lams[:, 0:1]
+            us.append(split(spec / (shift + lam)))
+        if step > 0:
+            p, c = chunks[step - 1]
+            u = us[step - 1]
+            r = halves(dot(by_hl, u[0], NT), 0) + dot(by_h, u[1], NT)
+            rs.append(split(jnp.concatenate([r * turns[p][0], r * turns[p][1]], axis=0)))
+            at = [BKXT + 64 * p + 32 * h + 16 * c for h in range(2)]
+            lines = jnp.concatenate([wide[k : k + 16, :] for k in at], axis=0)
+            bxs.append(halves(dot(lines, u[0]), 0) + dot(lines[:16], u[1]))
     bys = []
     for i in range(4):
         rh, rl = rs[i]
@@ -372,8 +401,7 @@
     qbuf[0:NZ] = got[pl.ds(0, NZ, stride=2), :].T
     qbuf[NZ : 2 * NZ] = got[pl.ds(1, NZ, stride=2), :].T
     sign = jnp.where(lanes((8, NZ), 0) % 2 == 0, 1.0, -1.0)
-    w = split(modes[...].T)
-    w = block_diag2(w[0]), block_diag2(w[1])
+    w = vertical_table(modes[...].T)
     for p in range(2):
         kxp = two(kxt, p)
         ends = []
@@ -399,16 +427,17 @@
                 ybuf[:, 8 * o : 8 * o + 8, p * NZ : (p + 1) * NZ] = back[
                     :, i * NZ : (i + 1) * NZ
                 ].reshape(H, 8, NZ)
-    kyp = two(ky)
+    table = ky[...]
     copies = []
     for g in range(8):
-        block = split(ybuf[4 * g : 4 * g + 4].reshape(4 * T, 2 * NZ))
-        modal = split(dot3(kyp, block))
-        res = dot3(modal, w)
-        near = res[:, :NZ]
-        far = res[:, NZ:]
-        obuf[4 * g : 4 * g + 4] = (near + far).reshape(4, T, NZ)
-        other = near - far
+        outs = []
+        for p in range(2):
+            block = ybuf[4 * g : 4 * g + 4, :, p * NZ : p * NZ + NZ].reshape(4 * T, NZ)
+            res = along_y(table, block)
+            outs.append(vertical(jnp.concatenate([res[:, :NZ], res[:, NZ:]], axis=0), w))
+        even, odd = outs
+        obuf[4 * g : 4 * g + 4] = (even + odd).reshape(4, T, NZ)
+        other = even - odd
         for i in range(4):
             obuf[63 - 4 * g - i] = other[T * i : T * i + T]
         for lo, hi in SENDS.get(g, ()):
@@ -453,7 +482,7 @@
             field,
             field,
             edge_shape,
-            jax.ShapeDtypeStruct(kron, BF16),
+            jax.ShapeDtypeStruct(kron[1:], BF16),
             jax.ShapeDtypeStruct((2, *kron), BF16),
             like(modes),
             like(eig),
@@ -467,7 +496,7 @@
             pltpu.VMEM((1, NZ), F32),
             pltpu.VMEM((2, *kron), BF16),
             pltpu.VMEM((H, T, 2 * NZ), F32),
-            pltpu.SemaphoreType.DMA((8,)),
+            pltpu.SemaphoreType.DMA((7,)),
         ],
         compiler_params=params,
         interpret=INTERPRET,

time: 48.8 us -> 46.3 us (0.949)
  Pallas kernels: 13.2 us -> 10.6 us
    pallas_call x1, Pallas kernels: 5.59 us -> 4.33 us  [shards(): pl.pallas_call(forward_kernel, out_shape=(field, field, edge_shape, jax.S...]
    pallas_call x1, Pallas kernels: 4.13 us -> 3.43 us  [shards(): pl.pallas_call(backward_kernel, out_shape=jax.ShapeDtypeStruct((T, T, NZ)...]
    pallas_call x1, Pallas kernels: 3.46 us -> 2.88 us  [shards(): pl.pallas_call(interface_kernel, out_shape=edge_shape, in_specs=[VMEM] *...]
where the time goes in v5:
time: 46.3 us; the launch traced here: 46.1 us
  blocking collectives  35.5 us (77%)
  Pallas kernels  10.6 us (23%)
    all_to_all x2, blocking collectives, exchange(): value = lax.all_to_all(value, AXES, split_axis=0, concat_axis=0, tiled=True)  35.5 us
    pallas_call x1, Pallas kernels, shards(): pl.pallas_call(forward_kernel, out_shape=(field, field, edge_shape, jax.S...  4.33 us
    pallas_call x1, Pallas kernels, shards(): pl.pallas_call(backward_kernel, out_shape=jax.ShapeDtypeStruct((T, T, NZ)...  3.43 us
    pallas_call x1, Pallas kernels, shards(): pl.pallas_call(interface_kernel, out_shape=edge_shape, in_specs=[VMEM] *...  2.88 us

profile of v5, /device:TPU:1, one launch (start us, length us, event | category | flops | bytes accessed | tf_op | source)
XLA Modules:
  0.0 46.1 jit_solution(17244093500927328721)
XLA Ops:
  0.0 4.3 %forward.1 = (f32[2,32,64,128]{3,2,1,0:T(8,128)S(1)}, f32[2,32,64,128]{3,2,1,0:T(8,128)S(1)}, f32[256,128]{1,0:T(8,128)S(1)}, bf16[256,256]{1,0:T(8,128)(2,1)S(1...) custom-call(f32[64,64,128]{2,1,0:T(8,128)} %src_in.1, ...), custom_call_target="tpu_custom_call" | custom-call | tf_op jit(solution)/shard_map/forward/pallas_call | solution.py:479
  4.3 21.3 %all_to_all.10 = f32[128,1,256]{2,1,0:T(1,128)S(1)} all-to-all(f32[128,1,256]{2,1,0:T(1,128)S(1)} %bitcast.9), channel_id=1, replica_groups=mesh['px'=16,'py'=8] {'px','py'}, dimensions={0} | all-to-all | bytes 262144 | tf_op jit(solution)/shard_map/all_to_all | solution.py:463
  25.6 2.9 %interface.1 = f32[256,128]{1,0:T(8,128)S(1)} custom-call(f32[256,128]{1,0:T(8,128)S(1)} %bitcast.7, f32[1,128]{1,0:T(1,128)S(1)} %get-tuple-element.17.eig, f32[552,256]{1,0:T(8,128)S(1)} %get-tuple-element.18.tab, bf16[3264,256]{1,0:T(8,128)(2,1)S(1)} %get-tuple-element.19.wide), custom_call_target="tpu_custom_call" | custom-call | tf_op jit(solution)/shard_map/interface/pallas_call | solution.py:505
  28.5 14.2 %all_to_all.11 = f32[128,1,256]{2,1,0:T(1,128)S(1)} all-to-all(f32[128,1,256]{2,1,0:T(1,128)S(1)} %bitcast.8), channel_id=1, replica_groups=mesh['px'=16,'py'=8] {'px','py'}, dimensions={0} | all-to-all | bytes 262144 | tf_op jit(solution)/shard_map/all_to_all | solution.py:463
  42.7 3.4 %backward.1 = f32[64,64,128]{2,1,0:T(8,128)} custom-call(f32[2,32,64,128]{3,2,1,0:T(8,128)S(1)} %get-tuple-element.14.coef, f32[2,32,64,128]{3,2,1,0:T(8,128)S(1)} %get-tuple-element.15.recip, f32[256,128]{1,0:T(8,128)S(1)} %bitcast.6, f32[128,128]{1,0:T(8,128)S(1)} %get-tuple-element.20.modes, bf16[256,256]{1,0:T(8,128)(2,1)S(1)} %get-tuple-element.21.ky, ...), custom_call_target="tpu_custom_call" | custom-call | tf_op jit(solution)/shard_map/backward/pallas_call | solution.py:515

commit v6 on v5

--- a/solution.py
+++ b/solution.py
@@ -75,12 +75,9 @@
     m2 = (sx[:, None] * np.sin(phase)) @ SINE[:, ORDER_A]
     m12 = np.concatenate(np_split(np.concatenate([m1, m2], axis=1)), axis=1)
     lam_x = 2.0 - 2.0 * np.cos(np.pi * al / NX)
-    lam_h, lam_l = np_split(lam_x)
-    rest = lam_x - lam_h.astype(np.float64) - lam_l.astype(np.float64)
     bkx_h, bkx_l = np_split(bkx)
-    lams = np.stack([lam_h, lam_l, np_split(rest)[0]], axis=1)
     bkx_all = np.zeros((NX, 128), jnp.bfloat16)
-    for i, part in enumerate((bkx_h, bkx_l, bkx_h, lams)):
+    for i, part in enumerate((bkx_h, bkx_l, bkx_h)):
         bkx_all[:, 16 * i : 16 * i + part.shape[1]] = part
     bkxt = np.stack([pair(bkx[512 * p : 512 * p + 512].T) for p in range(2)])
     px = np.arange(PX // 2)
@@ -100,12 +97,13 @@
     bkxt = bkxt.reshape(2, 2, 16, 2, 256).transpose(0, 1, 3, 2, 4)
     tr = np.stack([np.concatenate([tr[2 * p], tr[2 * p + 1]], axis=1) for p in range(2)])
     small, rowtab, ysel = tile_tables()
-    lam_y = np.concatenate([lam_y.reshape(2, 256), np.zeros((6, 256), np.float32)])
+    lams = [lam_y.reshape(2, 256), lam_x.astype(np.float32).reshape(4, 256)]
+    lams = np.concatenate([*lams, np.zeros((2, 256), np.float32)])
     flat = lambda parts: np.concatenate([t.reshape(-1, 256) for t in parts])
-    return flat([small, rowtab, tz, tr, lam_y]), flat([cyl, m12, bkx_all, bys, bkxt, ysel])
-
-
-SMALL, ROWTAB, TZ, TR, LAM_Y = 0, 192, 256, 288, 544
+    return flat([small, rowtab, lams, tz, tr]), flat([cyl, m12, bkx_all, bys, bkxt, ysel])
+
+
+SMALL, ROWTAB, LAMS, TZ, TR = 0, 192, 256, 264, 296
 CYL, M12, BKX, BYS, BKXT, YSEL = 0, 1024, 2048, 2560, 3072, 3200
 
 
@@ -164,8 +162,8 @@
 
 def forward_kernel(
     src_in, mass_in, modes_in, eig_in, tab_in, wide_in,
-    coef, recip, edges, ky, kxt, modes, eig, tab, wide,
-    src, mass, kx, ybuf, sems,
+    coef, recip, edges, ky, kxt, modes, tab, wide, scale,
+    src, mass, eig, kx, ybuf, sems,
 ):
     jobs = [(tab_in.at[:TZ], tab.at[:TZ]), (eig_in, eig), (mass_in, mass), (modes_in, modes)]
     jobs += [(src_in, src), (wide_in, wide), (tab_in.at[TZ:], tab.at[TZ:])]
@@ -194,6 +192,16 @@
         for p in range(2):
             for j in range(H):
                 recip[p, j, 8 * o : 8 * o + 8, :] = 1.0 / (base + float(LAM_T[2 * j + p]))
+    mode = lax.axis_index("px") * PY + lax.axis_index("py")
+    mu = jnp.sum(jnp.where(lanes((1, NZ), 1) == mode, eig_row, 0.0), axis=1, keepdims=True)
+    shift = jnp.concatenate([tab[LAMS : LAMS + 1, :], tab[LAMS + 1 : LAMS + 2, :]], axis=1) + mu
+    for i in range(8):
+        at = LAMS + 2 + i // 2
+        row = tab[at : at + 1, NZ * (i % 2) : NZ * (i % 2) + NZ]
+        lam = jnp.broadcast_to(row, (NZ, NZ)).T
+        for j in range(4):
+            cols = slice(NZ * j, NZ * j + NZ)
+            scale[NZ * i : NZ * i + NZ, cols] = 1.0 / (shift[:, cols] + lam)
     copies[2].wait()
     copies[3].wait()
     mass_col = jnp.broadcast_to(mass[...], (NZ, NZ)).T
@@ -260,11 +268,9 @@
     return pltpu.roll(m, T, 1)
 
 
-def interface_kernel(got, eig, tab, wide, out, xbuf):
+def interface_kernel(got, tab, wide, scale, out, xbuf):
     block = lambda at: wide[at : at + 256, :]
     cyl = [(block(CYL + 512 * i), block(CYL + 512 * i + 256)) for i in range(2)]
-    mode = lax.axis_index("px") * PY + lax.axis_index("py")
-    mu = jnp.sum(jnp.where(lanes((1, NZ), 1) == mode, eig[...], 0.0), axis=1, keepdims=True)
     lane = lanes((NZ, NZ), 1)
     low = lane < T
     low32 = low[: 2 * PX]
@@ -305,8 +311,6 @@
     ]
     by_lh = jnp.concatenate([by_l, by_h], axis=0)
     by_hl = jnp.concatenate([by_h, by_l], axis=0)
-    lam_y = jnp.concatenate([tab[LAM_Y : LAM_Y + 1, :], tab[LAM_Y + 1 : LAM_Y + 2, :]], axis=1)
-    shift = lam_y + mu
     chunks = [(p, c) for p in range(2) for c in range(2)]
     m = [block(M12 + 512 * p + 256 * c) for p, c in chunks]
     starts = []
@@ -318,13 +322,6 @@
         starts.append((jnp.concatenate([eh, eh], axis=0), el))
         th, tl = t1h[PX * p : PX * p + PX], t1l[PX * p : PX * p + PX]
         weights.append(jnp.concatenate([by_h, th, th, tl, pad], axis=0))
-    zs = []
-    for i, (p, c) in enumerate(chunks):
-        zz = dot(m[i], starts[p][0]) + dot(m[i][:, :NZ], starts[p][1])
-        turn = tab[TZ + 16 * p : TZ + 16 * p + 16, :][None]
-        zz = (zz.reshape(16, 16, 256) * turn).reshape(256, 256)
-        zs.append(split(zz[:, :NZ] + zz[:, NZ:]))
-    us, bxs, rs = [], [], []
     turns = [
         [
             jnp.concatenate([tab[TR + NZ * p : TR + NZ * p + NZ, NZ * j : NZ * j + NZ]] * 2, axis=1)
@@ -332,29 +329,59 @@
         ]
         for p in range(2)
     ]
-    for step in range(5):
-        if step < 4:
-            p, c = chunks[step]
-            zh, zl = zs[step]
-            bk = wide[BKX + 256 * p : BKX + 256 * p + 256, NZ * c : NZ * c + NZ]
-            spec = dot(jnp.concatenate([zh, bk], axis=1), weights[p])
-            spec += dot(jnp.concatenate([zh, zl], axis=1), by_lh)
-            lams = bk[:, 48:51].astype(F32)
-            lam = (lams[:, 2:3] + lams[:, 1:2]) + lams[:, 0:1]
-            us.append(split(spec / (shift + lam)))
-        if step > 0:
-            p, c = chunks[step - 1]
-            u = us[step - 1]
-            r = halves(dot(by_hl, u[0], NT), 0) + dot(by_h, u[1], NT)
-            rs.append(split(jnp.concatenate([r * turns[p][0], r * turns[p][1]], axis=0)))
-            at = [BKXT + 64 * p + 32 * h + 16 * c for h in range(2)]
-            lines = jnp.concatenate([wide[k : k + 16, :] for k in at], axis=0)
-            bxs.append(halves(dot(lines, u[0]), 0) + dot(lines[:16], u[1]))
-    bys = []
-    for i in range(4):
+    zs, us, bxs, rs, bys = {}, {}, {}, {}, {}
+
+    def enter(i):
+        p, c = chunks[i]
+        zz = dot(m[i], starts[p][0]) + dot(m[i][:, :NZ], starts[p][1])
+        turn = tab[TZ + 16 * p : TZ + 16 * p + 16, :][None]
+        zz = (zz.reshape(16, 16, 256) * turn).reshape(256, 256)
+        zs[i] = split(zz[:, :NZ] + zz[:, NZ:])
+
+    def scaled(i):
+        p, c = chunks[i]
+        zh, zl = zs[i]
+        bk = wide[BKX + 256 * p : BKX + 256 * p + 256, NZ * c : NZ * c + NZ]
+        spec = dot(jnp.concatenate([zh, zl], axis=1), by_lh)
+        spec += dot(jnp.concatenate([zh, bk], axis=1), weights[p])
+        us[i] = split(spec * scale[512 * p + 256 * c : 512 * p + 256 * c + 256, :])
+
+    def lines_of(i):
+        p, c = chunks[i]
+        at = [BKXT + 64 * p + 32 * h + 16 * c for h in range(2)]
+        lines = jnp.concatenate([wide[k : k + 16, :] for k in at], axis=0)
+        bxs[i] = halves(dot(lines, us[i][0]), 0) + dot(lines[:16], us[i][1])
+
+    def rows_of(i):
+        p, c = chunks[i]
+        r = halves(dot(by_hl, us[i][0], NT), 0) + dot(by_h, us[i][1], NT)
+        rs[i] = split(jnp.concatenate([r * turns[p][0], r * turns[p][1]], axis=0))
+
+    def leave(i):
         rh, rl = rs[i]
         both = dot(rh, m[i])
-        bys.append(both[:, :NZ] + both[:, NZ:] + dot(rl, m[i][:, :NZ]))
+        bys[i] = both[:, :NZ] + both[:, NZ:] + dot(rl, m[i][:, :NZ])
+
+    enter(0)
+    enter(1)
+    enter(2)
+    enter(3)
+    scaled(0)
+    scaled(1)
+    rows_of(0)
+    lines_of(0)
+    scaled(2)
+    rows_of(1)
+    lines_of(1)
+    scaled(3)
+    rows_of(2)
+    lines_of(2)
+    rows_of(3)
+    lines_of(3)
+    leave(0)
+    leave(1)
+    leave(2)
+    leave(3)
     back_x = [bxs[0] + bxs[1], bxs[2] + bxs[3]]
     back_y = [bys[0] + bys[1], bys[2] + bys[3]]
     back_y = [y[:NZ] + swap(y[NZ:]) for y in back_y]
@@ -476,7 +503,7 @@
         pltpu.with_memory_space_constraint(jnp.asarray(v), pltpu.HBM)
         for v in (source, mass, modes, eig, tab, wide)
     ]
-    coef, recip, edges, ky, kxt, modes, eig, tab, wide = pl.pallas_call(
+    coef, recip, edges, ky, kxt, modes, tab, wide, scale = pl.pallas_call(
         forward_kernel,
         out_shape=(
             field,
@@ -485,14 +512,15 @@
             jax.ShapeDtypeStruct(kron[1:], BF16),
             jax.ShapeDtypeStruct((2, *kron), BF16),
             like(modes),
-            like(eig),
             like(tab),
             like(wide),
+            jax.ShapeDtypeStruct((NX, NY), F32),
         ),
         in_specs=[HBM] * 6,
         out_specs=[VMEM] * 9,
         scratch_shapes=[
             pltpu.VMEM((T, T, NZ), F32),
+            pltpu.VMEM((1, NZ), F32),
             pltpu.VMEM((1, NZ), F32),
             pltpu.VMEM((2, *kron), BF16),
             pltpu.VMEM((H, T, 2 * NZ), F32),
@@ -511,7 +539,7 @@
         compiler_params=params,
         interpret=INTERPRET,
         name="interface",
-    )(exchange(edges), eig, tab, wide)
+    )(exchange(edges), tab, wide, scale)
     return pl.pallas_call(
         backward_kernel,
         out_shape=jax.ShapeDtypeStruct((T, T, NZ), F32),

time: 46.3 us -> 46.1 us (level)
  no operation moved by 1% of the time
where the time goes in v6:
time: 46.1 us; the launch traced here: 46 us
  blocking collectives  35.5 us (77%)
  Pallas kernels  10.5 us (23%)
    all_to_all x2, blocking collectives, exchange(): value = lax.all_to_all(value, AXES, split_axis=0, concat_axis=0, tiled=True)  35.5 us
    pallas_call x1, Pallas kernels, shards(): pl.pallas_call(forward_kernel, out_shape=(field, field, edge_shape, jax.S...  4.36 us
    pallas_call x1, Pallas kernels, shards(): pl.pallas_call(backward_kernel, out_shape=jax.ShapeDtypeStruct((T, T, NZ)...  3.35 us
    pallas_call x1, Pallas kernels, shards(): pl.pallas_call(interface_kernel, out_shape=edge_shape, in_specs=[VMEM] *...  2.83 us

profile of v6, /device:TPU:1, one launch (start us, length us, event | category | flops | bytes accessed | tf_op | source)
XLA Modules:
  0.0 46.0 jit_solution(17077645670649656089)
XLA Ops:
  0.0 4.4 %forward.1 = (f32[2,32,64,128]{3,2,1,0:T(8,128)S(1)}, f32[2,32,64,128]{3,2,1,0:T(8,128)S(1)}, f32[256,128]{1,0:T(8,128)S(1)}, bf16[256,256]{1,0:T(8,128)(2,1)S(1...) custom-call(f32[64,64,128]{2,1,0:T(8,128)} %src_in.1, ...), custom_call_target="tpu_custom_call" | custom-call | tf_op jit(solution)/shard_map/forward/pallas_call | solution.py:506
  4.4 21.3 %all_to_all.10 = f32[128,1,256]{2,1,0:T(1,128)S(1)} all-to-all(f32[128,1,256]{2,1,0:T(1,128)S(1)} %bitcast.9), channel_id=1, replica_groups=mesh['px'=16,'py'=8] {'px','py'}, dimensions={0} | all-to-all | bytes 262144 | tf_op jit(solution)/shard_map/all_to_all | solution.py:490
  25.7 2.8 %interface.1 = f32[256,128]{1,0:T(8,128)S(1)} custom-call(f32[256,128]{1,0:T(8,128)S(1)} %bitcast.7, f32[552,256]{1,0:T(8,128)S(1)} %get-tuple-element.17.tab, bf16[3264,256]{1,0:T(8,128)(2,1)S(1)} %get-tuple-element.18.wide, f32[1024,512]{1,0:T(8,128)S(1)} %get-tuple-element.19.scale), custom_call_target="tpu_custom_call" | custom-call | tf_op jit(solution)/shard_map/interface/pallas_call | solution.py:533
  28.5 14.2 %all_to_all.11 = f32[128,1,256]{2,1,0:T(1,128)S(1)} all-to-all(f32[128,1,256]{2,1,0:T(1,128)S(1)} %bitcast.8), channel_id=1, replica_groups=mesh['px'=16,'py'=8] {'px','py'}, dimensions={0} | all-to-all | bytes 262144 | tf_op jit(solution)/shard_map/all_to_all | solution.py:490
  42.7 3.3 %backward.1 = f32[64,64,128]{2,1,0:T(8,128)} custom-call(f32[2,32,64,128]{3,2,1,0:T(8,128)S(1)} %get-tuple-element.14.coef, f32[2,32,64,128]{3,2,1,0:T(8,128)S(1)} %get-tuple-element.15.recip, f32[256,128]{1,0:T(8,128)S(1)} %bitcast.6, f32[128,128]{1,0:T(8,128)S(1)} %get-tuple-element.20.modes, bf16[256,256]{1,0:T(8,128)(2,1)S(1)} %get-tuple-element.21.ky, ...), custom_call_target="tpu_custom_call" | custom-call | tf_op jit(solution)/shard_map/backward/pallas_call | solution.py:543

commit v7 on v6

--- a/solution.py
+++ b/solution.py
@@ -268,6 +268,9 @@
     return pltpu.roll(m, T, 1)
 
 
+PAIRS = ((0, 1), (2, 3), (7, 6), (5, 4))
+
+
 def interface_kernel(got, tab, wide, scale, out, xbuf):
     block = lambda at: wide[at : at + 256, :]
     cyl = [(block(CYL + 512 * i), block(CYL + 512 * i + 256)) for i in range(2)]
@@ -281,17 +284,17 @@
     gx = got[pl.ds(0, NZ, stride=2), :]
     gy = got[pl.ds(1, NZ, stride=2), :]
 
-    mirror = swap(turned(gx))
-    xbuf[...] = jnp.where(low, gx + mirror, swap(gx - mirror))
+    swapped_x = swap(gx)
+    xbuf[...] = jnp.where(low, gx + turned(swapped_x), swapped_x - turned(gx))
     tiles = []
-    for q in range(4):
+    for places in PAIRS:
         rows = []
-        for i in range(2):
-            d = xbuf[pl.ds(2 * q + i, PX, stride=PY), :]
+        for i, at in enumerate(places):
+            d = xbuf[pl.ds(at, PX, stride=PY), :]
             other = swap(d)
             rows.append(jnp.concatenate([d, other] if i == 0 else [other, d], axis=0))
         tiles.append(jnp.where(low32, rows[0], rows[1]))
-    flipped = [sign_b * swap(tiles[3 - q]) for q in range(2)]
+    flipped = [sign_b * t for t in tiles[2:]]
     line_e = jnp.concatenate([tiles[q] + flipped[q] for q in range(2)], axis=1)
     line_o = jnp.concatenate([tiles[q] - flipped[q] for q in range(2)], axis=1)
     t1 = jnp.concatenate(
@@ -384,24 +387,21 @@
     leave(3)
     back_x = [bxs[0] + bxs[1], bxs[2] + bxs[3]]
     back_y = [bys[0] + bys[1], bys[2] + bys[3]]
-    back_y = [y[:NZ] + swap(y[NZ:]) for y in back_y]
 
     bx = jnp.concatenate(back_x, axis=0)
     we = dot3(split(bx[:, : NY // 2]), cyl[0], NT)
     wo = dot3(split(bx[:, NY // 2 :]), cyl[1], NT)
     near = we + wo
     far = we - wo
-    for q in range(4):
-        if q < 2:
-            t = near[:, q * NZ : (q + 1) * NZ]
-        else:
-            t = swap(sign_b * far[:, (3 - q) * NZ : (4 - q) * NZ])
+    for q, (first, second) in enumerate(PAIRS):
+        t = (near if q < 2 else far)[:, q % 2 * NZ : q % 2 * NZ + NZ]
+        t = t if q < 2 else sign_b * t
         s0 = t[:PX] + t[PX:]
         s1 = t[:PX] - t[PX:]
-        xbuf[pl.ds(2 * q, PX, stride=PY), :] = jnp.where(low16, s0, swap(s1))
-        xbuf[pl.ds(2 * q + 1, PX, stride=PY), :] = jnp.where(low16, swap(s0), s1)
+        xbuf[pl.ds(first, PX, stride=PY), :] = jnp.where(low16, s0, swap(s1))
+        xbuf[pl.ds(second, PX, stride=PY), :] = jnp.where(low16, swap(s0), s1)
     w = xbuf[...]
-    other = swap(gx)
+    other = swapped_x
     own = jnp.where(
         low,
         jnp.concatenate([gx[:PY], other[:-PY]], axis=0),
@@ -409,10 +409,11 @@
     )
     out[pl.ds(0, NZ, stride=2), :] = jnp.where(low, w, turned(w)) + own
 
-    near = back_y[0] + back_y[1]
-    far = back_y[0] - back_y[1]
-    near = jnp.where(low64, near[:T], swap(near[T:]))
-    far = sign_a * jnp.where(low64, far[:T], swap(far[T:]))
+    near, far = (
+        jnp.where(low64, y[:T] + swap(y[NZ : NZ + T]), swap(y[T:NZ]) + y[NZ + T :])
+        for y in (back_y[0] + back_y[1], back_y[0] - back_y[1])
+    )
+    far = sign_a * far
     w = jnp.concatenate([near, turned(jnp.concatenate([far, far], axis=0))[:T]], axis=0)
     row = lanes((NZ, NZ), 0) % PY
     other = swap(gy)

time: 46.1 us -> 46 us (level)
  no operation moved by 1% of the time
where the time goes in v7:
time: 46 us; the launch traced here: 45.8 us
  blocking collectives  35.5 us (77%)
  Pallas kernels  10.3 us (22%)
    all_to_all x2, blocking collectives, exchange(): value = lax.all_to_all(value, AXES, split_axis=0, concat_axis=0, tiled=True)  35.5 us
    pallas_call x1, Pallas kernels, shards(): pl.pallas_call(forward_kernel, out_shape=(field, field, edge_shape, jax.S...  4.36 us
    pallas_call x1, Pallas kernels, shards(): pl.pallas_call(backward_kernel, out_shape=jax.ShapeDtypeStruct((T, T, NZ)...  3.34 us
    pallas_call x1, Pallas kernels, shards(): pl.pallas_call(interface_kernel, out_shape=edge_shape, in_specs=[VMEM] *...  2.64 us

profile of v7, /device:TPU:1, one launch (start us, length us, event | category | flops | bytes accessed | tf_op | source)
XLA Modules:
  0.0 45.8 jit_solution(17278297528734391568)
XLA Ops:
  0.0 4.4 %forward.1 = (f32[2,32,64,128]{3,2,1,0:T(8,128)S(1)}, f32[2,32,64,128]{3,2,1,0:T(8,128)S(1)}, f32[256,128]{1,0:T(8,128)S(1)}, bf16[256,256]{1,0:T(8,128)(2,1)S(1...) custom-call(f32[64,64,128]{2,1,0:T(8,128)} %src_in.1, ...), custom_call_target="tpu_custom_call" | custom-call | tf_op jit(solution)/shard_map/forward/pallas_call | solution.py:507
  4.4 21.3 %all_to_all.10 = f32[128,1,256]{2,1,0:T(1,128)S(1)} all-to-all(f32[128,1,256]{2,1,0:T(1,128)S(1)} %bitcast.9), channel_id=1, replica_groups=mesh['px'=16,'py'=8] {'px','py'}, dimensions={0} | all-to-all | bytes 262144 | tf_op jit(solution)/shard_map/all_to_all | solution.py:491
  25.7 2.6 %interface.1 = f32[256,128]{1,0:T(8,128)S(1)} custom-call(f32[256,128]{1,0:T(8,128)S(1)} %bitcast.7, f32[552,256]{1,0:T(8,128)S(1)} %get-tuple-element.17.tab, bf16[3264,256]{1,0:T(8,128)(2,1)S(1)} %get-tuple-element.18.wide, f32[1024,512]{1,0:T(8,128)S(1)} %get-tuple-element.19.scale), custom_call_target="tpu_custom_call" | custom-call | tf_op jit(solution)/shard_map/interface/pallas_call | solution.py:534
  28.3 14.2 %all_to_all.11 = f32[128,1,256]{2,1,0:T(1,128)S(1)} all-to-all(f32[128,1,256]{2,1,0:T(1,128)S(1)} %bitcast.8), channel_id=1, replica_groups=mesh['px'=16,'py'=8] {'px','py'}, dimensions={0} | all-to-all | bytes 262144 | tf_op jit(solution)/shard_map/all_to_all | solution.py:491
  42.5 3.3 %backward.1 = f32[64,64,128]{2,1,0:T(8,128)} custom-call(f32[2,32,64,128]{3,2,1,0:T(8,128)S(1)} %get-tuple-element.14.coef, f32[2,32,64,128]{3,2,1,0:T(8,128)S(1)} %get-tuple-element.15.recip, f32[256,128]{1,0:T(8,128)S(1)} %bitcast.6, f32[128,128]{1,0:T(8,128)S(1)} %get-tuple-element.20.modes, bf16[256,256]{1,0:T(8,128)(2,1)S(1)} %get-tuple-element.21.ky, ...), custom_call_target="tpu_custom_call" | custom-call | tf_op jit(solution)/shard_map/backward/pallas_call | solution.py:544
